TPU v7x, 128 devices: a whole 4x4x4 slice. The times are simulated.
128 devices in a mesh: row: 16 (over x, y), col: 8 (over z, core).
Axes of the slice: x: 4, y: 4, z: 4, core: 2. Of those that a mesh axis runs over, the one named last changes fastest.
Arguments:
- matrix: float32 [32768, 8192], P('row', 'col'), may hold values from -40 to 40
Outputs:
- upper: float32 [256, 8192], P('row', 'col')
- reduced: float32 [32768, 8192], P('row', 'col')
All inputs are finite; a program needn't handle non-finite values.
Results may differ from a plain program's by a relative error of at most 0.0003.
Values sent between devices are 32-bit elements; how exact they have to be, the bound alone decides.
No kernel may reach another device: no remote copies, remote signals or barrier semaphores. Data moves between devices by JAX's collectives and lax.ppermute only.
A program may use at most 128 MiB of HBM per device.

v0:
```python
import jax
import jax.numpy as jnp
from jax import lax
from jax.sharding import Mesh
from jax.sharding import PartitionSpec as P

PANEL = 256
COL = ("z", "c")
EXACT = lax.Precision.HIGHEST
HIGH = lax.Precision.HIGH


def dot(left, right, contract, precision):
    return lax.dot_general(
        left, right, (contract, ((), ())), precision=precision, preferred_element_type=jnp.float32
    )


def from_everyone(shard, axis):
    copies = jnp.broadcast_to(shard, (lax.axis_size(axis), *shard.shape))
    return lax.all_to_all(copies, axis, 0, 0, tiled=True)


def spread_panel(panel, col):
    half = panel.shape[0] // 2
    low, high = panel[:half], panel[half:]
    first = col == 0
    low = jnp.where(first, low, 0.0)
    high = jnp.where(first, high, 0.0)
    low = low + lax.ppermute(low, COL, [(0, 2)])
    high = high + lax.ppermute(high, COL, [(0, 6)])
    low = low + lax.ppermute(low, COL, [(0, 6), (2, 4)])
    high = high + lax.ppermute(high, COL, [(0, 2), (6, 4)])
    swap = [(0, 1), (2, 3), (4, 5), (6, 7)]
    low = low + lax.ppermute(low, COL, swap)
    high = high + lax.ppermute(high, COL, swap)
    return jnp.concatenate([low, high], axis=0)


def shards(matrix):
    rows = lax.axis_size("row")
    total_rows = matrix.shape[0] * rows
    col = lax.axis_index(COL)
    me = lax.axis_index("row")
    own_panel = matrix[:, :PANEL]

    gram = dot(own_panel, own_panel, ((0,), (0,)), EXACT)
    piece = lax.all_to_all(gram.reshape(rows, PANEL // rows, PANEL), "row", 0, 0, tiled=True).sum(0)
    piece = from_everyone(piece, COL)[0]
    gram = from_everyone(piece, "row").reshape(PANEL, PANEL)
    lower = jnp.linalg.cholesky(gram)
    inverse = jax.scipy.linalg.solve_triangular(lower, jnp.eye(PANEL, dtype=jnp.float32), lower=True)

    panel = spread_panel(own_panel, col)
    product = dot(matrix, panel, ((0,), (0,)), HIGH)
    width = product.shape[0] // rows
    share = lax.all_to_all(product.reshape(rows, width, PANEL), "row", 0, 0, tiled=True).sum(0)
    product = from_everyone(share, "row").reshape(rows * width, PANEL)

    block = PANEL // rows
    mine = lax.dynamic_slice(inverse, (me * block, 0), (block, PANEL))
    upper = dot(mine, product, ((1,), (1,)), EXACT)
    coefficients = dot(product, inverse, ((1,), (1,)), EXACT)
    weights = dot(coefficients, inverse, ((1,), (0,)), EXACT)
    scale = jnp.sqrt(jnp.float32(total_rows))
    holds = col == 0
    weights = jnp.concatenate(
        [jnp.where(holds, -scale * inverse, weights[:PANEL]), weights[PANEL:]], axis=0
    )
    is_panel = (lax.broadcasted_iota(jnp.int32, matrix.shape, 1) < PANEL) & holds
    reduced = jnp.where(is_panel, 0.0, matrix) - dot(panel, weights, ((1,), (1,)), HIGH)
    return (upper, reduced)


def solution(mesh):
    finer = Mesh(mesh.devices.reshape(mesh.shape["row"], 4, 2), ("row", *COL))
    return jax.shard_map(
        shards,
        mesh=finer,
        in_specs=(P("row", COL),),
        out_specs=(P("row", COL), P("row", COL)),
        check_vma=False,
    )
```

profile of v0, /device:TPU:2, one launch (start us, length us, event | category | flops | bytes accessed | tf_op | source)
XLA Modules:
  0.0 175.6 jit_solution(16417759113621441790)
XLA Ops:
  0.6 1.7 slice_select_fusion.1
  2.3 3.9 %collective-permute-start = (f32[1024,256]{1,0:T(8,128)S(1)}, f32[1024,256]{1,0:T(8,128)S(1)}, u32[]{:S(2)}, u32[]{:S(2)}) collective-permute-start(f32[1024,256]{1,0:T(8,128)S(1)} %get-tuple-element.20), channel_id=1, source_target_pairs={{0,2},{8,10},{16,18},{24,26},{32,34},{40,42},{48,50},{56,58},{64,6... | collective-permute-start | bytes 3145736 | tf_op jit(solution)/shard_map/ppermute | solution.py:30
  6.2 2.8 %collective-permute-start.3 = (f32[1024,256]{1,0:T(8,128)S(1)}, f32[1024,256]{1,0:T(8,128)S(1)}, u32[]{:S(2)}, u32[]{:S(2)}) collective-permute-start(f32[1024,256]{1,0:T(8,128)S(1)} %get-tuple-element.21), channel_id=1, source_target_pairs={{0,6},{8,14},{16,22},{24,30},{32,38},{40,46},{48,54},{56,62},{64,7... | collective-permute-start | bytes 3145736 | tf_op jit(solution)/shard_map/ppermute | solution.py:31
  9.1 9.4 %collective-permute-done = f32[1024,256]{1,0:T(8,128)S(1)} collective-permute-done((f32[1024,256]{1,0:T(8,128)S(1)}, f32[1024,256]{1,0:T(8,128)S(1)}, u32[]{:S(2)}, u32[]{:S(2)}) %collective-permute-start) | collective-permute-done | bytes 1048608 | tf_op jit(solution)/shard_map/ppermute | solution.py:30
  18.5 0.1 add.50
  18.6 2.3 %collective-permute-start.1 = (f32[1024,256]{1,0:T(8,128)S(1)}, f32[1024,256]{1,0:T(8,128)}, u32[]{:S(2)}, u32[]{:S(2)}) collective-permute-start(f32[1024,256]{1,0:T(8,128)S(1)} %add.50), channel_id=1, source_target_pairs={{0,6},{2,4},{8,14},{10,12},{16,22},{18,20},{24,30},{26,28},{32,38}... | collective-permute-start | bytes 3145736 | tf_op jit(solution)/shard_map/ppermute | solution.py:32
  20.9 0.4 collective-permute-done.3
  21.3 0.1 add.53
  21.5 5.0 %collective-permute-start.4 = (f32[1024,256]{1,0:T(8,128)S(1)}, f32[1024,256]{1,0:T(8,128)}, u32[]{:S(2)}, u32[]{:S(2)}) collective-permute-start(f32[1024,256]{1,0:T(8,128)S(1)} %add.53), channel_id=1, source_target_pairs={{0,2},{6,4},{8,10},{14,12},{16,18},{22,20},{24,26},{30,28},{32,34}... | collective-permute-start | bytes 3145736 | tf_op jit(solution)/shard_map/ppermute | solution.py:33
  26.5 6.5 %fusion = f32[256,256]{1,0:T(8,128)} fusion(f32[2048,1024]{1,0:T(8,128)} %param.1), kind=kOutput, calls=%fused_computation.4 | convolution fusion | flops 1610612736 | bytes 2359296 | tf_op jit(solution)/shard_map/dot_general | solution.py:14
  32.9 7.5 %all-to-all-start = ((f32[16,16,256]{2,1,0:T(8,128)}), f32[16,16,256]{2,1,0:T(8,128)S(1)}, u32[]{:S(2)}, u32[]{:S(2)}) async-start(f32[16,16,256]{2,1,0:T(8,128)} %bitcast), calls=%async_computation | async-start | bytes 524288 | tf_op jit(solution)/shard_map/all_to_all | solution.py:48
  40.4 1.4 add.51
  41.8 2.3 %collective-permute-start.2 = (f32[1024,256]{1,0:T(8,128)S(1)}, f32[1024,256]{1,0:T(8,128)}, u32[]{:S(2)}, u32[]{:S(2)}) collective-permute-start(f32[1024,256]{1,0:T(8,128)S(1)} %add.51), channel_id=1, source_target_pairs={{0,1},{2,3},{4,5},{6,7},{8,9},{10,11},{12,13},{14,15},{16,17},{18,... | collective-permute-start | bytes 3145736 | tf_op jit(solution)/shard_map/ppermute | solution.py:35
  44.0 1.7 add.54
  45.7 2.3 %collective-permute-start.5 = (f32[1024,256]{1,0:T(8,128)S(1)}, f32[1024,256]{1,0:T(8,128)}, u32[]{:S(2)}, u32[]{:S(2)}) collective-permute-start(f32[1024,256]{1,0:T(8,128)S(1)} %add.54), channel_id=1, source_target_pairs={{0,1},{2,3},{4,5},{6,7},{8,9},{10,11},{12,13},{14,15},{16,17},{18,... | collective-permute-start | bytes 3145736 | tf_op jit(solution)/shard_map/ppermute | solution.py:36
  48.1 8.5 %all_to_all.25 = f32[8,16,256]{2,1,0:T(8,128)S(1)} all-to-all(f32[8,16,256]{2,1,0:T(8,128)S(1)} %broadcast_in_dim.20), channel_id=1, replica_groups=mesh['row'=16,'z'=4,'c'=2] {'z','c'}, dimensions={0} | all-to-all | bytes 262144 | tf_op jit(solution)/shard_map/all_to_all | solution.py:21
  56.6 0.7 broadcast_in_dim.21
  57.3 7.2 %all-to-all-start.2 = ((f32[16,16,256]{2,1,0:T(8,128)}), f32[16,16,256]{2,1,0:T(8,128)S(1)}, u32[]{:S(2)}, u32[]{:S(2)}) async-start(f32[16,16,256]{2,1,0:T(8,128)} %broadcast_in_dim.21), calls=%async_computation.2 | async-start | bytes 524288 | tf_op jit(solution)/shard_map/all_to_all | solution.py:21
  64.6 0.7 iota_compare_fusion
  65.2 6.1 %all-to-all-done.2 = f32[16,16,256]{2,1,0:T(8,128)S(1)} async-done(((f32[16,16,256]{2,1,0:T(8,128)}), f32[16,16,256]{2,1,0:T(8,128)S(1)}, u32[]{:S(2)}, u32[]{:S(2)}) %all-to-all-start.2) | async-done | bytes 262176 | tf_op jit(solution)/shard_map/all_to_all | solution.py:21
  71.4 0.1 copy.4
  71.6 11.7 %cholesky.50 = f32[128,128]{1,0:T(8,128)S(1)} custom-call(f32[128,128]{1,0:T(8,128)S(1)} %cholesky.118), custom_call_target="Cholesky" | custom-call | tf_op jit(solution)/shard_map/jit(cholesky)/cholesky | solution.py:51
  83.3 9.8 %custom-call.15 = f32[1,128,128]{1,2,0:T(8,128)S(1)} custom-call(f32[1,128,128]{2,1,0:T(8,128)S(1)} %get-tuple-element.25), custom_call_target="InvertDiagBlocksLowerTriangular" | custom-call | tf_op jit(solution)/shard_map/jit(cholesky)/cholesky | solution.py:51
  93.2 1.4 add.52
  94.5 1.4 add.55
  95.9 5.9 %fusion.3 = f32[1024,256]{0,1:T(8,128)S(1)} fusion(f32[2048,1024]{1,0:T(8,128)} %param.1, f32[1024,256]{1,0:T(8,128)S(1)} %add.55, f32[1024,256]{1,0:T(8,128)S(1)} %add.52), kind=kOutput, calls=%fused_computation.7 | convolution fusion | flops 3221749760 | bytes 11534336 | tf_op jit(solution)/shard_map/dot_general | solution.py:14
  101.9 1.3 copy.5
  103.2 5.3 %all-to-all-start.3 = ((f32[16,64,256]{2,1,0:T(8,128)}), f32[16,64,256]{2,1,0:T(8,128)S(1)}, u32[]{:S(2)}, u32[]{:S(2)}) async-start(f32[16,64,256]{2,1,0:T(8,128)} %bitcast.46), calls=%async_computation.3 | async-start | bytes 2097152 | tf_op jit(solution)/shard_map/all_to_all | solution.py:57
  108.5 1.0 constant_dynamic-update-slice_fusion
  109.6 1.1 convolution_subtract_fusion.1
  110.7 11.7 %cholesky.105 = f32[128,128]{1,0:T(8,128)S(1)} custom-call(f32[128,128]{1,0:T(8,128)S(1)} %convolution_subtract_fusion.1), custom_call_target="Cholesky" | custom-call | tf_op jit(solution)/shard_map/jit(cholesky)/cholesky | solution.py:51
  122.4 0.7 compare_reduce_fusion
  124.4 1.0 select_select_fusion
  125.5 1.1 broadcast_in_dim.23
  126.5 7.2 %all-to-all-start.4 = ((f32[16,64,256]{2,1,0:T(8,128)}), f32[16,64,256]{2,1,0:T(8,128)S(1)}, u32[]{:S(2)}, u32[]{:S(2)}) async-start(f32[16,64,256]{2,1,0:T(8,128)} %broadcast_in_dim.23), calls=%async_computation.4 | async-start | bytes 2097152 | tf_op jit(solution)/shard_map/all_to_all | solution.py:21
  133.8 5.3 %while.1 = (s32[]{:T(128)}, f32[256,256]{1,0:T(8,128)S(1)}, s32[2,2]{1,0:T(2,128)S(1)}, f32[2,128,128]{2,1,0:T(8,128)}, s32[]{:T(128)}) while((s32[]{:T(128)}, f32[256,256]{1,0:T(8,128)S(1)}, s32[2,2]{1,0:T(2,128)S(1)}, f32[2,128,128]{2,1,0:T(8,128)}, s32[]{:T(128)}) %tuple.28), condition=%wide.while_cond, body=%wide.while_body.sunk | while | flops 2 | bytes 132205 | solution.py:52
  133.8 0.7 fusion.37
  134.5 2.0 %bitcast_dynamic-update-slice_fusion.2 = f32[2,128,128]{2,1,0:T(8,128)} fusion(f32[2,128,128]{2,1,0:T(8,128)} %get-tuple-element.67, s32[]{:T(128)S(6)} %copy.11, f32[256,256]{1,0:T(8,128)S(1)} %get-tuple-element.70, s32[]{:T(128)} %bitcast.42, s32[]{:T(128)} %bitcast.43), kind=kLoop, calls=%fused_computation.clone.1 | loop fusion | bytes 132100 | tf_op jit(solution)/shard_map/jit(_solve_triangular)/triangular_solve
  136.5 0.7 fusion.37
  137.1 2.0 %bitcast_dynamic-update-slice_fusion.2 = f32[2,128,128]{2,1,0:T(8,128)} fusion(f32[2,128,128]{2,1,0:T(8,128)} %get-tuple-element.67, s32[]{:T(128)S(6)} %copy.11, f32[256,256]{1,0:T(8,128)S(1)} %get-tuple-element.70, s32[]{:T(128)} %bitcast.42, s32[]{:T(128)} %bitcast.43), kind=kLoop, calls=%fused_computation.clone.1 | loop fusion | bytes 132100 | tf_op jit(solution)/shard_map/jit(_solve_triangular)/triangular_solve
  139.1 21.1 %custom-call.16 = f32[2,128,128]{1,2,0:T(8,128)} custom-call(f32[2,128,128]{2,1,0:T(8,128)} %get-tuple-element.9), custom_call_target="InvertDiagBlocksLowerTriangular" | custom-call | tf_op jit(solution)/shard_map/jit(_solve_triangular)/triangular_solve | solution.py:52
  160.2 1.1 fusion.10
  161.3 1.0 convolution_subtract_fusion
  162.4 1.1 fusion.13
  163.5 1.0 fusion.8
  164.6 1.0 fusion.9
  165.7 1.6 fusion.18
  167.3 8.3 %select_subtract_fusion = f32[2048,1024]{1,0:T(8,128)} fusion(f32[2048,1024]{1,0:T(8,128)} %param.1, pred[1024]{0:T(1024)(128)(4,1)S(1)} %fusion.20, f32[1024,256]{1,0:T(8,128)S(1)} %add.55, f32[1024,256]{1,0:T(8,128)S(1)} %add.52, f32[768,256]{1,0:T(8,128)S(1)} %slice.87, f32[256,256]{1,0:T(8,128)S(1)} %slice_select_fusion.2), kind=kOutput, calls=%fused_computation.2 | convolution fusion | flops 3226206208 | bytes 19923968 | tf_op jit(solution)/shard_map/dot_general | solution.py:14
  (30 shorter events, 0.4 us)
Async XLA Ops:
  2.3 16.1 %collective-permute-start = (f32[1024,256]{1,0:T(8,128)S(1)}, f32[1024,256]{1,0:T(8,128)S(1)}, u32[]{:S(2)}, u32[]{:S(2)}) collective-permute-start(f32[1024,256]{1,0:T(8,128)S(1)} %get-tuple-element.20), channel_id=1, source_target_pairs={{0,2},{8,10},{16,18},{24,26},{32,34},{40,42},{48,50},{56,58},{64,6... | collective-permute-start | bytes 3145736 | tf_op jit(solution)/shard_map/ppermute | solution.py:30
  6.2 15.1 %collective-permute-start.3 = (f32[1024,256]{1,0:T(8,128)S(1)}, f32[1024,256]{1,0:T(8,128)S(1)}, u32[]{:S(2)}, u32[]{:S(2)}) collective-permute-start(f32[1024,256]{1,0:T(8,128)S(1)} %get-tuple-element.21), channel_id=1, source_target_pairs={{0,6},{8,14},{16,22},{24,30},{32,38},{40,46},{48,54},{56,62},{64,7... | collective-permute-start | bytes 3145736 | tf_op jit(solution)/shard_map/ppermute | solution.py:31
  18.6 21.8 %collective-permute-start.1 = (f32[1024,256]{1,0:T(8,128)S(1)}, f32[1024,256]{1,0:T(8,128)}, u32[]{:S(2)}, u32[]{:S(2)}) collective-permute-start(f32[1024,256]{1,0:T(8,128)S(1)} %add.50), channel_id=1, source_target_pairs={{0,6},{2,4},{8,14},{10,12},{16,22},{18,20},{24,30},{26,28},{32,38}... | collective-permute-start | bytes 3145736 | tf_op jit(solution)/shard_map/ppermute | solution.py:32
  21.5 22.6 %copy-start = (f32[1024,256]{1,0:T(8,128)}, f32[1024,256]{1,0:T(8,128)S(1)}, u32[]{:S(2)}) copy-start(f32[1024,256]{1,0:T(8,128)S(1)} %add.53) | copy-start | bytes 3145732
  21.5 22.6 %collective-permute-start.4 = (f32[1024,256]{1,0:T(8,128)S(1)}, f32[1024,256]{1,0:T(8,128)}, u32[]{:S(2)}, u32[]{:S(2)}) collective-permute-start(f32[1024,256]{1,0:T(8,128)S(1)} %add.53), channel_id=1, source_target_pairs={{0,2},{6,4},{8,10},{14,12},{16,18},{22,20},{24,26},{30,28},{32,34}... | collective-permute-start | bytes 3145736 | tf_op jit(solution)/shard_map/ppermute | solution.py:33
  32.9 15.1 %all-to-all-start = ((f32[16,16,256]{2,1,0:T(8,128)}), f32[16,16,256]{2,1,0:T(8,128)S(1)}, u32[]{:S(2)}, u32[]{:S(2)}) async-start(f32[16,16,256]{2,1,0:T(8,128)} %bitcast), calls=%async_computation | async-start | bytes 524288 | tf_op jit(solution)/shard_map/all_to_all | solution.py:48
  41.8 51.4 %collective-permute-start.2 = (f32[1024,256]{1,0:T(8,128)S(1)}, f32[1024,256]{1,0:T(8,128)}, u32[]{:S(2)}, u32[]{:S(2)}) collective-permute-start(f32[1024,256]{1,0:T(8,128)S(1)} %add.51), channel_id=1, source_target_pairs={{0,1},{2,3},{4,5},{6,7},{8,9},{10,11},{12,13},{14,15},{16,17},{18,... | collective-permute-start | bytes 3145736 | tf_op jit(solution)/shard_map/ppermute | solution.py:35
  45.7 48.8 %collective-permute-start.5 = (f32[1024,256]{1,0:T(8,128)S(1)}, f32[1024,256]{1,0:T(8,128)}, u32[]{:S(2)}, u32[]{:S(2)}) collective-permute-start(f32[1024,256]{1,0:T(8,128)S(1)} %add.54), channel_id=1, source_target_pairs={{0,1},{2,3},{4,5},{6,7},{8,9},{10,11},{12,13},{14,15},{16,17},{18,... | collective-permute-start | bytes 3145736 | tf_op jit(solution)/shard_map/ppermute | solution.py:36
  57.3 14.0 %all-to-all-start.2 = ((f32[16,16,256]{2,1,0:T(8,128)}), f32[16,16,256]{2,1,0:T(8,128)S(1)}, u32[]{:S(2)}, u32[]{:S(2)}) async-start(f32[16,16,256]{2,1,0:T(8,128)} %broadcast_in_dim.21), calls=%async_computation.2 | async-start | bytes 524288 | tf_op jit(solution)/shard_map/all_to_all | solution.py:21
  71.5 21.6 %copy-start.2 = (f32[256,256]{1,0:T(8,128)}, f32[256,256]{1,0:T(8,128)S(1)}, u32[]{:S(2)}) copy-start(f32[256,256]{1,0:T(8,128)S(1)} %fusion.7) | copy-start | bytes 786436
  103.2 22.2 %all-to-all-start.3 = ((f32[16,64,256]{2,1,0:T(8,128)}), f32[16,64,256]{2,1,0:T(8,128)S(1)}, u32[]{:S(2)}, u32[]{:S(2)}) async-start(f32[16,64,256]{2,1,0:T(8,128)} %bitcast.46), calls=%async_computation.3 | async-start | bytes 2097152 | tf_op jit(solution)/shard_map/all_to_all | solution.py:57
  122.4 2.0 %copy-start.1 = (f32[256,256]{1,0:T(8,128)}, f32[256,256]{1,0:T(8,128)S(1)}, u32[]{:S(2)}) copy-start(f32[256,256]{1,0:T(8,128)S(1)} %get-tuple-element.23) | copy-start | bytes 786436
  126.5 37.0 %all-to-all-start.4 = ((f32[16,64,256]{2,1,0:T(8,128)}), f32[16,64,256]{2,1,0:T(8,128)S(1)}, u32[]{:S(2)}, u32[]{:S(2)}) async-start(f32[16,64,256]{2,1,0:T(8,128)} %broadcast_in_dim.23), calls=%async_computation.4 | async-start | bytes 2097152 | tf_op jit(solution)/shard_map/all_to_all | solution.py:21
where the time goes:
time: 177 us; the launch traced here: 176 us
  other arithmetic  64.6 us (36%)
  starting transfers between devices  45.9 us (26%)
  matrix products  29.7 us (17%)
  waiting for transfers between devices  16 us (9%)
  local copies, waits for them, and re-layouts  8.69 us (5%)
  blocking collectives  8.49 us (5%)
  between operations  2.17 us (1%)
    another operation x6, other arithmetic, shards(): lower = jnp.linalg.cholesky(gram)  34 us
    dot_general x6, matrix products, dot(): lax.dot_general(left, right, (contract, ((), ())), precision=precision, p...  24.3 us
    another operation x3, other arithmetic, shards(): jax.scipy.linalg.solve_triangular(lower, jnp.eye(PANEL, dtype=jnp.float32...  22.1 us
    all_to_all x2, starting transfers between devices, from_everyone(): return lax.all_to_all(copies, axis, 0, 0, tiled=True)  14.5 us
    ppermute x1, waiting for transfers between devices, spread_panel(): low = low + lax.ppermute(low, COL, [(0, 2)])  9.38 us
    all_to_all x1, blocking collectives, from_everyone(): return lax.all_to_all(copies, axis, 0, 0, tiled=True)  8.49 us
    all_to_all x1, starting transfers between devices, shards(): lax.all_to_all(gram.reshape(rows, PANEL // rows, PANEL), 'row', 0, 0, til...  7.48 us
    all_to_all x2, waiting for transfers between devices, from_everyone(): return lax.all_to_all(copies, axis, 0, 0, tiled=True)  6.12 us
  transfers between devices with their start and end apart: 10, of which 3 were waited for; matrix products, arithmetic and copies ran while one was open for 45% of the time, Pallas kernels for 0%

commit v1 on v0

v1 whole, which is shorter than its diff:
```python
import jax
import jax.numpy as jnp
from jax import lax
from jax.experimental import pallas as pl
from jax.experimental.pallas import tpu as pltpu
from jax.sharding import Mesh
from jax.sharding import PartitionSpec as P

PANEL = 256
COL = ("z", "c")
EXACT = lax.Precision.HIGHEST
F32 = jnp.float32
BLOCK, SUB, LANES = 32, 8, 128
ROWS = 512


def eliminate(strip, start):
    groups = BLOCK // SUB
    row_id = lax.broadcasted_iota(jnp.int32, (SUB, LANES), 0)
    lane_id = lax.broadcasted_iota(jnp.int32, (SUB, LANES), 1)
    half, lane0 = divmod(start, LANES)
    tiles = [list(t) for t in strip]
    diagonal = [jnp.zeros((SUB, LANES), F32) for _ in range(groups)]
    panel = 16
    for p in range(0, BLOCK, panel):
        g0 = p // SUB
        cols = {
            k: {g: jnp.broadcast_to(tiles[g][half][:, lane0 + k : lane0 + k + 1], (SUB, LANES)) for g in range(g0, groups)}
            for k in range(p, p + panel)
        }
        for j in range(p, p + panel):
            gj, sj = divmod(j, SUB)
            pivot = jnp.broadcast_to(cols[j][gj][sj : sj + 1], (SUB, LANES))
            diagonal[gj] = jnp.where(row_id == sj, pivot, diagonal[gj])
            inverse = 1.0 / pivot
            factor = {g: cols[j][g] * inverse for g in range(gj, groups)}
            factor[gj] = jnp.where(row_id > sj, factor[gj], 0.0)
            for k in range(j + 1, p + panel):
                row = jnp.broadcast_to(cols[k][gj][sj : sj + 1], (SUB, LANES))
                for g in range(gj, groups):
                    cols[k][g] = cols[k][g] - factor[g] * row
            for h in range(2):
                source = tiles[gj][h][sj : sj + 1]
                if h == half:
                    source = jnp.where(lane_id[0:1] == lane0 + j, 1.0, source)
                row = jnp.broadcast_to(source, (SUB, LANES))
                for g in range(gj, groups):
                    tile = tiles[g][h]
                    if h == half:
                        tile = jnp.where((lane_id == lane0 + j) & ((row_id > sj) if g == gj else True), 0.0, tile)
                    tiles[g][h] = tile - factor[g] * row
                if h == half:
                    tiles[gj][h] = jnp.where((lane_id == lane0 + j) & (row_id == sj), 1.0, tiles[gj][h])
    out = []
    for g in range(groups):
        r = lax.rsqrt(diagonal[g])
        r = r * (1.5 - 0.5 * diagonal[g] * r * r)
        above = (lane_id > lane0 + g * SUB + row_id) & (lane_id < lane0 + BLOCK)
        tiles[g][half] = jnp.where(above, 0.0, tiles[g][half])
        out.append([tiles[g][h] * r for h in range(2)])
    return out


def factor(work, inverse):
    n = work.shape[0]
    col_id = lax.broadcasted_iota(jnp.int32, (BLOCK, n), 1)
    for start in range(0, n, BLOCK):
        strip = [
            [work[start + SUB * g : start + SUB * (g + 1), LANES * h : LANES * (h + 1)] for h in range(2)]
            for g in range(BLOCK // SUB)
        ]
        done = eliminate(strip, start)
        rows = jnp.concatenate([jnp.concatenate(t, axis=1) for t in done], axis=0)
        inverse[start : start + BLOCK, :] = jnp.where(col_id < start + BLOCK, rows, 0.0)
        after = start + BLOCK
        for lo, hi in ((after, after + BLOCK), (after + BLOCK, n)):
            if lo >= n or lo >= hi:
                continue
            base = work[lo:hi, :]
            ids = lax.broadcasted_iota(jnp.int32, (hi - lo, n), 1)
            base = jnp.where((ids >= start) & (ids < after), 0.0, base)
            step = dot(rows[:, lo:hi], rows, ((0,), (0,)), EXACT)
            work[lo:hi, :] = base - step


def dot(left, right, contract, precision=None):
    return lax.dot_general(
        left, right, (contract, ((), ())), precision=precision, preferred_element_type=F32
    )


def split(value):
    high = value.astype(jnp.bfloat16)
    return high, (value - high.astype(F32)).astype(jnp.bfloat16)


NN = ((1,), (0,))


def split_dot(left, right):
    return dot(left[0], right[0], NN) + (dot(left[0], right[1], NN) + dot(left[1], right[0], NN))


def prepare_kernel(matrix, high, low):
    high[...], low[...] = split(matrix[...])


def product_kernel(low, low_more, high, high_more, matrix_high, matrix_low, out, panel_high, panel_low):
    half = low.shape[0]
    cols = matrix_high.shape[1]
    for first, more, start in ((low, low_more, 0), (high, high_more, half)):
        part = slice(start, start + half)
        panel = first[...] + more[...]
        panel_high[part], panel_low[part] = split(panel)
        turned = panel.T
        pieces = split(turned)
        for c in range(0, cols, PANEL):
            here = slice(c, c + PANEL)
            value = split_dot(pieces, (matrix_high[part, here], matrix_low[part, here]))
            out[:, here] = value if start == 0 else out[:, here] + value
        value = dot(turned, panel, NN, EXACT)
        out[:, cols:] = value if start == 0 else out[:, cols:] + value


def finish_kernel(place, gathered, panel_high, panel_low, matrix, upper, out, work, inverse, coeff, coeff_low, held, arrived, left):
    blocks = matrix.shape[0] // ROWS
    cols = matrix.shape[1]
    scale = float(matrix.shape[0] * (PANEL // upper.shape[0])) ** 0.5

    def fetch(b):
        part = slice(b * ROWS, b * ROWS + ROWS)
        return pltpu.make_async_copy(matrix.at[part], held.at[part], arrived.at[b])

    def send(b):
        part = slice(b * ROWS, b * ROWS + ROWS)
        return pltpu.make_async_copy(held.at[part], out.at[part], left.at[b])

    for b in range(blocks):
        fetch(b).start()
    holds = place[0] == 1
    work[...] = gathered[:, cols:]
    factor(work, inverse)
    lower = split(inverse[...])
    turned = inverse[...].T
    upward = split(turned)
    height = upper.shape[0]
    mine = pl.ds(pl.multiple_of(place[1] * height, height), height)
    for c in range(0, cols, PANEL):
        here = slice(c, c + PANEL)
        work[...] = split_dot(lower, split(gathered[:, here]))
        upper[:, here] = work[mine, :]
        weights = split_dot(upward, split(work[...]))
        if c == 0:
            weights = jnp.where(holds, -scale * turned, weights)
        coeff[:, here], coeff_low[:, here] = split(weights)

    for b in range(blocks):
        part = slice(b * ROWS, b * ROWS + ROWS)
        fetch(b).wait()
        panel = (panel_high[part], panel_low[part])
        for c in range(0, cols, PANEL):
            here = slice(c, c + PANEL)
            change = split_dot(panel, (coeff[:, here], coeff_low[:, here]))
            value = held[part, here]
            if c == 0:
                value = jnp.where(holds, 0.0, value)
            held[part, here] = value - change
        send(b).start()
    for b in range(blocks):
        send(b).wait()


VMEM = pl.BlockSpec(memory_space=pltpu.VMEM)
SMEM = pl.BlockSpec(memory_space=pltpu.SMEM)
HBM = pl.BlockSpec(memory_space=pltpu.HBM)


def prepare(matrix):
    shape = jax.ShapeDtypeStruct(matrix.shape, jnp.bfloat16)
    block = pl.BlockSpec((ROWS // 2, matrix.shape[1]), lambda i: (i, 0))
    return pl.pallas_call(
        prepare_kernel,
        grid=(2 * matrix.shape[0] // ROWS,),
        out_shape=(shape, shape),
        in_specs=[block],
        out_specs=(block, block),
        cost_estimate=pl.CostEstimate(flops=3 * 10**9, bytes_accessed=16 << 20, transcendentals=0),
    )(matrix)


def products(low, low_more, high, high_more, pieces):
    rows, cols = pieces[0].shape
    narrow = jax.ShapeDtypeStruct((rows, PANEL), jnp.bfloat16)
    return pl.pallas_call(
        product_kernel,
        out_shape=(jax.ShapeDtypeStruct((PANEL, cols + PANEL), F32), narrow, narrow),
        in_specs=[VMEM] * 6,
        out_specs=[VMEM] * 3,
        compiler_params=pltpu.CompilerParams(vmem_limit_bytes=32 << 20),
        cost_estimate=pl.CostEstimate(flops=5 * 10**9, bytes_accessed=16 << 20, transcendentals=0),
    )(low, low_more, high, high_more, *pieces)


def finish(place, gathered, panel_high, panel_low, matrix, height):
    rows, cols = matrix.shape
    return pl.pallas_call(
        finish_kernel,
        out_shape=(
            jax.ShapeDtypeStruct((height, cols), F32),
            jax.ShapeDtypeStruct(matrix.shape, F32),
        ),
        in_specs=[SMEM] + [VMEM] * 3 + [HBM],
        out_specs=[VMEM, HBM],
        scratch_shapes=[
            pltpu.VMEM((PANEL, PANEL), F32),
            pltpu.VMEM((PANEL, PANEL), F32),
            pltpu.VMEM((PANEL, cols), jnp.bfloat16),
            pltpu.VMEM((PANEL, cols), jnp.bfloat16),
            pltpu.VMEM(matrix.shape, F32),
            pltpu.SemaphoreType.DMA((rows // ROWS,)),
            pltpu.SemaphoreType.DMA((rows // ROWS,)),
        ],
        compiler_params=pltpu.CompilerParams(vmem_limit_bytes=50 << 20),
        cost_estimate=pl.CostEstimate(flops=8 * 10**9, bytes_accessed=24 << 20, transcendentals=0),
    )(place, gathered, panel_high, panel_low, matrix)


def from_everyone(shard, axis):
    copies = jnp.broadcast_to(shard, (lax.axis_size(axis), *shard.shape))
    return lax.all_to_all(copies, axis, 0, 0, tiled=True)


def sum_at_owner(shard, axis):
    count = lax.axis_size(axis)
    tiles = shard.reshape(count, shard.shape[0] // count, shard.shape[1])
    return lax.all_to_all(tiles, axis, 0, 0, tiled=True).sum(0)


def shards(matrix):
    holds = lax.axis_index(COL) == 0
    half = matrix.shape[0] // 2
    own_low, own_high = lax.optimization_barrier((matrix[:half, :PANEL], matrix[half:, :PANEL]))
    swap = [(0, 1), (2, 3), (4, 5), (6, 7)]
    low = lax.ppermute(own_low, COL, [(0, 2)])
    high = lax.ppermute(own_high, COL, [(0, 6)])
    low_too = lax.ppermute(own_low, COL, [(0, 6)])
    high_too = lax.ppermute(own_high, COL, [(0, 2)])
    pieces = prepare(matrix)
    low_relay = lax.ppermute(low, COL, [(2, 4)])
    high_relay = lax.ppermute(high, COL, [(6, 4)])
    low = jnp.where(holds, own_low, low + low_too + low_relay)
    high = jnp.where(holds, own_high, high + high_too + high_relay)
    low_more = lax.ppermute(low, COL, swap)
    high_more = lax.ppermute(high, COL, swap)
    product, panel_high, panel_low = products(low, low_more, high, high_more, pieces)
    share = sum_at_owner(product, "row")
    gathered = from_everyone(share, "row").reshape(product.shape)
    place = jnp.stack([holds.astype(jnp.int32), lax.axis_index("row").astype(jnp.int32)])
    upper, reduced = finish(place, gathered, panel_high, panel_low, matrix, share.shape[0])
    return (upper, reduced)


def solution(mesh):
    finer = Mesh(mesh.devices.reshape(mesh.shape["row"], 4, 2), ("row", *COL))
    return jax.shard_map(
        shards,
        mesh=finer,
        in_specs=(P("row", COL),),
        out_specs=(P("row", COL), P("row", COL)),
        check_vma=False,
    )
```

time: 177 us -> 121 us (0.68)
  the two profiles are of different devices: /device:TPU:2 before, /device:TPU:32 now
where the time goes in v1:
time: 121 us; the launch traced here: 120 us
  waiting for transfers between devices  36.6 us (30%)
  Pallas kernels  30.7 us (25%)
  blocking collectives  21.1 us (17%)
  starting transfers between devices  17.3 us (14%)
  local copies, waits for them, and re-layouts  9.23 us (8%)
  other arithmetic  4.4 us (4%)
    all_to_all x1, blocking collectives, sum_at_owner(): return lax.all_to_all(tiles, axis, 0, 0, tiled=True).sum(0)  21.1 us
    pallas_call x1, Pallas kernels, finish(): pl.pallas_call(finish_kernel, out_shape=(jax.ShapeDtypeStruct((height, co...  15.2 us
    all_to_all x1, waiting for transfers between devices, from_everyone(): return lax.all_to_all(copies, axis, 0, 0, tiled=True)  14.2 us
    ppermute x1, waiting for transfers between devices, shards(): low = lax.ppermute(own_low, COL, [(0, 2)])  12.1 us
    pallas_call x1, Pallas kernels, prepare(): pl.pallas_call(prepare_kernel, grid=(2 * matrix.shape[0] // ROWS,), out_s...  8.94 us
    ppermute x1, waiting for transfers between devices, shards(): low_relay = lax.ppermute(low, COL, [(2, 4)])  8.38 us
    pallas_call x1, Pallas kernels, products(): pl.pallas_call(product_kernel, out_shape=(jax.ShapeDtypeStruct((PANEL, co...  6.58 us
    unnamed x16, local copies, waits for them, and re-layouts  6.36 us
  transfers between devices with their start and end apart: 9, of which 4 were waited for; matrix products, arithmetic and copies ran while one was open for 4% of the time, Pallas kernels for 7%

profile of v1, /device:TPU:32, one launch (start us, length us, event | category | flops | bytes accessed | tf_op | source)
XLA Modules:
  0.0 120.2 jit_solution(1712849606526994300)
XLA Ops:
  0.6 1.7 %fusion = (f32[1024,256]{1,0:T(8,128)S(1)}, f32[1024,256]{1,0:T(8,128)S(1)}) fusion(f32[2048,1024]{1,0:T(8,128)} %matrix.3), kind=kLoop, calls=%fused_computation.3 | loop fusion | bytes 4194304 | tf_op jit(solution)/shard_map/slice | solution.py:242
  2.3 0.0 copy-start.6
  2.3 1.3 %collective-permute-start = (f32[1024,256]{1,0:T(8,128)S(1)}, f32[1024,256]{1,0:T(8,128)S(1)}, u32[]{:S(2)}, u32[]{:S(2)}) collective-permute-start(f32[1024,256]{1,0:T(8,128)S(1)} %get-tuple-element.9), channel_id=1, source_target_pairs={{0,2},{8,10},{16,18},{24,26},{32,34},{40,42},{48,50},{56,58},{64,6... | collective-permute-start | bytes 3145736 | tf_op jit(solution)/shard_map/ppermute | solution.py:244
  3.6 1.7 %collective-permute-start.4 = (f32[1024,256]{1,0:T(8,128)S(1)}, f32[1024,256]{1,0:T(8,128)}, u32[]{:S(2)}, u32[]{:S(2)}) collective-permute-start(f32[1024,256]{1,0:T(8,128)S(1)} %get-tuple-element.10), channel_id=1, source_target_pairs={{0,6},{8,14},{16,22},{24,30},{32,38},{40,46},{48,54},{56,62},{64,7... | collective-permute-start | bytes 3145736 | tf_op jit(solution)/shard_map/ppermute | solution.py:245
  5.3 1.7 %collective-permute-start.1 = (f32[1024,256]{1,0:T(8,128)S(1)}, f32[1024,256]{1,0:T(8,128)}, u32[]{:S(2)}, u32[]{:S(2)}) collective-permute-start(f32[1024,256]{1,0:T(8,128)S(1)} %get-tuple-element.9), channel_id=1, source_target_pairs={{0,6},{8,14},{16,22},{24,30},{32,38},{40,46},{48,54},{56,62},{64,7... | collective-permute-start | bytes 3145736 | tf_op jit(solution)/shard_map/ppermute | solution.py:246
  7.0 12.1 %collective-permute-done = f32[1024,256]{1,0:T(8,128)S(1)} collective-permute-done((f32[1024,256]{1,0:T(8,128)S(1)}, f32[1024,256]{1,0:T(8,128)S(1)}, u32[]{:S(2)}, u32[]{:S(2)}) %collective-permute-start) | collective-permute-done | bytes 1048608 | tf_op jit(solution)/shard_map/ppermute | solution.py:244
  19.0 0.0 copy-start.7
  19.0 2.3 %collective-permute-start.2 = (f32[1024,256]{1,0:T(8,128)S(1)}, f32[1024,256]{1,0:T(8,128)}, u32[]{:S(2)}, u32[]{:S(2)}) collective-permute-start(f32[1024,256]{1,0:T(8,128)S(1)} %collective-permute-done), channel_id=1, source_target_pairs={{2,4},{10,12},{18,20},{26,28},{34,36},{42,44},{50,52},{58,60},{66,... | collective-permute-start | bytes 3145736 | tf_op jit(solution)/shard_map/ppermute | solution.py:249
  21.3 1.3 %collective-permute-start.5 = (f32[1024,256]{1,0:T(8,128)S(1)}, f32[1024,256]{1,0:T(8,128)}, u32[]{:S(2)}, u32[]{:S(2)}) collective-permute-start(f32[1024,256]{1,0:T(8,128)S(1)} %get-tuple-element.10), channel_id=1, source_target_pairs={{0,2},{8,10},{16,18},{24,26},{32,34},{40,42},{48,50},{56,58},{64,6... | collective-permute-start | bytes 3145736 | tf_op jit(solution)/shard_map/ppermute | solution.py:247
  22.6 0.0 collective-permute-done.4
  22.6 1.6 %collective-permute-start.6 = (f32[1024,256]{1,0:T(8,128)}, f32[1024,256]{1,0:T(8,128)}, u32[]{:S(2)}, u32[]{:S(2)}) collective-permute-start(f32[1024,256]{1,0:T(8,128)} %collective-permute-done.4), channel_id=1, source_target_pairs={{6,4},{14,12},{22,20},{30,28},{38,36},{46,44},{54,52},{62,60},{70,... | collective-permute-start | bytes 3145736 | tf_op jit(solution)/shard_map/ppermute | solution.py:250
  24.2 0.0 collective-permute-done.1
  24.2 0.0 copy-done.7
  24.2 8.4 %collective-permute-done.2 = f32[1024,256]{1,0:T(8,128)} collective-permute-done((f32[1024,256]{1,0:T(8,128)S(1)}, f32[1024,256]{1,0:T(8,128)}, u32[]{:S(2)}, u32[]{:S(2)}) %collective-permute-start.2) | collective-permute-done | bytes 1048608 | tf_op jit(solution)/shard_map/ppermute | solution.py:249
  32.6 2.1 %add_select_fusion.1.low = f32[1024,256]{1,0:T(8,128)S(1)} fusion(f32[1024,256]{1,0:T(8,128)S(1)} %get-tuple-element.9, f32[1024,256]{1,0:T(8,128)} %collective-permute-done.2, f32[1024,256]{1,0:T(8,128)} %copy-done.7, f32[1024,256]{1,0:T(8,128)} %collective-permute-done.1, pred[]{:T(512)S(6)} %eq.3), kind=kLoop, calls=%fused_computation.1 | loop fusion | flops 786432 | bytes 5242881 | tf_op jit(solution)/shard_map/jit(_where)/select_n | solution.py:251
  34.7 1.4 %collective-permute-start.3 = (f32[1024,256]{1,0:T(8,128)S(1)}, f32[1024,256]{1,0:T(8,128)S(1)}, u32[]{:S(2)}, u32[]{:S(2)}) collective-permute-start(f32[1024,256]{1,0:T(8,128)S(1)} %add_select_fusion.1.low), channel_id=1, source_target_pairs={{0,1},{2,3},{4,5},{6,7},{8,9},{10,11},{12,13},{14,15},{16,17},{18,... | collective-permute-start | bytes 3145736 | tf_op jit(solution)/shard_map/ppermute | solution.py:253
  36.1 2.0 %collective-permute-done.5 = f32[1024,256]{1,0:T(8,128)} collective-permute-done((f32[1024,256]{1,0:T(8,128)S(1)}, f32[1024,256]{1,0:T(8,128)}, u32[]{:S(2)}, u32[]{:S(2)}) %collective-permute-start.5) | collective-permute-done | bytes 1048608 | tf_op jit(solution)/shard_map/ppermute | solution.py:247
  38.1 0.0 copy-done.6
  38.1 0.0 collective-permute-done.6
  38.1 2.1 %add_select_fusion.high = f32[1024,256]{1,0:T(8,128)S(1)} fusion(f32[1024,256]{1,0:T(8,128)} %copy-done.6, f32[1024,256]{1,0:T(8,128)} %collective-permute-done.6, f32[1024,256]{1,0:T(8,128)} %collective-permute-done.4, f32[1024,256]{1,0:T(8,128)} %collective-permute-done.5, pred[]{:T(512)S(6)} %eq.3), kind=kLoop, calls=%fused_computation | loop fusion | flops 786432 | bytes 5242881 | tf_op jit(solution)/shard_map/jit(_where)/select_n | solution.py:252
  40.2 2.3 %collective-permute-start.7 = (f32[1024,256]{1,0:T(8,128)S(1)}, f32[1024,256]{1,0:T(8,128)}, u32[]{:S(2)}, u32[]{:S(2)}) collective-permute-start(f32[1024,256]{1,0:T(8,128)S(1)} %add_select_fusion.high), channel_id=1, source_target_pairs={{0,1},{2,3},{4,5},{6,7},{8,9},{10,11},{12,13},{14,15},{16,17},{18,... | collective-permute-start | bytes 3145736 | tf_op jit(solution)/shard_map/ppermute | solution.py:254
  42.5 8.9 %shard_map.30 = (bf16[2048,1024]{1,0:T(8,128)(2,1)}, bf16[2048,1024]{1,0:T(8,128)(2,1)}) custom-call(f32[2048,1024]{1,0:T(8,128)} %matrix.3), custom_call_target="tpu_custom_call" | custom-call | flops 3000000000 | bytes 16777216 | tf_op jit(solution)/shard_map/pallas_call | solution.py:181
  51.4 0.0 collective-permute-done.3.low_more
  51.4 0.0 collective-permute-done.7.high_more
  51.4 0.0 copy-start
  51.5 2.2 %copy-done = bf16[2048,1024]{1,0:T(8,128)(2,1)S(1)} copy-done((bf16[2048,1024]{1,0:T(8,128)(2,1)S(1)}, bf16[2048,1024]{1,0:T(8,128)(2,1)}, u32[]{:S(2)}) %copy-start) | copy-done | bytes 4194328
  53.6 0.0 copy-start.1
  53.6 2.2 %copy-done.1 = bf16[2048,1024]{1,0:T(8,128)(2,1)S(1)} copy-done((bf16[2048,1024]{1,0:T(8,128)(2,1)S(1)}, bf16[2048,1024]{1,0:T(8,128)(2,1)}, u32[]{:S(2)}) %copy-start.1) | copy-done | bytes 4194328
  55.8 6.6 %shard_map.31 = (f32[256,1280]{1,0:T(8,128)S(1)}, bf16[2048,256]{1,0:T(8,128)(2,1)S(1)}, bf16[2048,256]{1,0:T(8,128)(2,1)S(1)}) custom-call(f32[1024,256]{1,0:T(8,128)S(1)} %add_select_fusion.1.low, f32[1024,256]{1,0:T(8,128)S(1)} %collective-permute-done.3.low_more, f32[1024,256]{1,0:T(8,128)S(1)} %add_select_fusion.high, ...), custom_call_target="tpu_custom_call" | custom-call | flops 5000000000 | bytes 16777216 | tf_op jit(solution)/shard_map/pallas_call | solution.py:194
  62.4 0.0 copy-start.2
  62.4 1.0 copy-done.2
  63.4 0.0 copy-start.4
  63.4 1.0 copy-done.4
  64.4 0.0 copy-start.3
  64.4 0.0 copy-start.5
  64.4 21.1 %all_to_all.10 = f32[16,16,1280]{2,1,0:T(8,128)S(1)} all-to-all(f32[16,16,1280]{2,1,0:T(8,128)S(1)} %bitcast.5), channel_id=1, replica_groups=mesh['row'=16,'z'=4,'c'=2] {'row'}, dimensions={0} | all-to-all | bytes 2621440 | tf_op jit(solution)/shard_map/all_to_all | solution.py:236
  85.5 0.1 reduce_sum.9
  85.5 1.2 broadcast_in_dim.3
  86.7 3.9 %all-to-all-start.1 = ((f32[16,16,1280]{2,1,0:T(8,128)}), f32[16,16,1280]{2,1,0:T(8,128)S(1)}, u32[]{:S(2)}, u32[]{:S(2)}) async-start(f32[16,16,1280]{2,1,0:T(8,128)} %broadcast_in_dim.3), calls=%async_computation.1 | async-start | bytes 2621440 | tf_op jit(solution)/shard_map/all_to_all | solution.py:230
  90.6 0.1 pad_add_fusion.place
  90.7 14.2 %all-to-all-done.1 = f32[16,16,1280]{2,1,0:T(8,128)S(1)} async-done(((f32[16,16,1280]{2,1,0:T(8,128)}), f32[16,16,1280]{2,1,0:T(8,128)S(1)}, u32[]{:S(2)}, u32[]{:S(2)}) %all-to-all-start.1) | async-done | bytes 1310752 | tf_op jit(solution)/shard_map/all_to_all | solution.py:230
  104.9 0.0 copy-done.3
  104.9 0.0 copy-done.5
  104.9 15.2 %shard_map.32 = (f32[16,1024]{1,0:T(8,128)}, f32[2048,1024]{1,0:T(8,128)}) custom-call(s32[2]{0:T(128)S(1)} %pad_add_fusion.place, f32[256,1280]{1,0:T(8,128)S(1)} %bitcast.4, bf16[2048,256]{1,0:T(8,128)(2,1)S(1)} %copy-done.3, bf16[2048,256]{1,0:T(8,128)(2,1)S(1)} %copy-done.5, f32[2048,1024]{1,0:T(8,128)} %matrix.3), custom_call_target="tpu_custom_call" | custom-call | flops 8000000000 | bytes 25165824 | tf_op jit(solution)/shard_map/pallas_call | solution.py:206
Async XLA Ops:
  2.3 35.8 %copy-start.6 = (f32[1024,256]{1,0:T(8,128)}, f32[1024,256]{1,0:T(8,128)S(1)}, u32[]{:S(2)}) copy-start(f32[1024,256]{1,0:T(8,128)S(1)} %get-tuple-element.10) | copy-start | bytes 3145732
  2.3 16.7 %collective-permute-start = (f32[1024,256]{1,0:T(8,128)S(1)}, f32[1024,256]{1,0:T(8,128)S(1)}, u32[]{:S(2)}, u32[]{:S(2)}) collective-permute-start(f32[1024,256]{1,0:T(8,128)S(1)} %get-tuple-element.9), channel_id=1, source_target_pairs={{0,2},{8,10},{16,18},{24,26},{32,34},{40,42},{48,50},{56,58},{64,6... | collective-permute-start | bytes 3145736 | tf_op jit(solution)/shard_map/ppermute | solution.py:244
  3.6 18.9 %collective-permute-start.4 = (f32[1024,256]{1,0:T(8,128)S(1)}, f32[1024,256]{1,0:T(8,128)}, u32[]{:S(2)}, u32[]{:S(2)}) collective-permute-start(f32[1024,256]{1,0:T(8,128)S(1)} %get-tuple-element.10), channel_id=1, source_target_pairs={{0,6},{8,14},{16,22},{24,30},{32,38},{40,46},{48,54},{56,62},{64,7... | collective-permute-start | bytes 3145736 | tf_op jit(solution)/shard_map/ppermute | solution.py:245
  5.3 18.9 %collective-permute-start.1 = (f32[1024,256]{1,0:T(8,128)S(1)}, f32[1024,256]{1,0:T(8,128)}, u32[]{:S(2)}, u32[]{:S(2)}) collective-permute-start(f32[1024,256]{1,0:T(8,128)S(1)} %get-tuple-element.9), channel_id=1, source_target_pairs={{0,6},{8,14},{16,22},{24,30},{32,38},{40,46},{48,54},{56,62},{64,7... | collective-permute-start | bytes 3145736 | tf_op jit(solution)/shard_map/ppermute | solution.py:246
  19.0 5.2 %copy-start.7 = (f32[1024,256]{1,0:T(8,128)}, f32[1024,256]{1,0:T(8,128)S(1)}, u32[]{:S(2)}) copy-start(f32[1024,256]{1,0:T(8,128)S(1)} %collective-permute-done) | copy-start | bytes 3145732
  19.0 13.6 %collective-permute-start.2 = (f32[1024,256]{1,0:T(8,128)S(1)}, f32[1024,256]{1,0:T(8,128)}, u32[]{:S(2)}, u32[]{:S(2)}) collective-permute-start(f32[1024,256]{1,0:T(8,128)S(1)} %collective-permute-done), channel_id=1, source_target_pairs={{2,4},{10,12},{18,20},{26,28},{34,36},{42,44},{50,52},{58,60},{66,... | collective-permute-start | bytes 3145736 | tf_op jit(solution)/shard_map/ppermute | solution.py:249
  21.3 16.8 %collective-permute-start.5 = (f32[1024,256]{1,0:T(8,128)S(1)}, f32[1024,256]{1,0:T(8,128)}, u32[]{:S(2)}, u32[]{:S(2)}) collective-permute-start(f32[1024,256]{1,0:T(8,128)S(1)} %get-tuple-element.10), channel_id=1, source_target_pairs={{0,2},{8,10},{16,18},{24,26},{32,34},{40,42},{48,50},{56,58},{64,6... | collective-permute-start | bytes 3145736 | tf_op jit(solution)/shard_map/ppermute | solution.py:247
  22.6 15.5 %collective-permute-start.6 = (f32[1024,256]{1,0:T(8,128)}, f32[1024,256]{1,0:T(8,128)}, u32[]{:S(2)}, u32[]{:S(2)}) collective-permute-start(f32[1024,256]{1,0:T(8,128)} %collective-permute-done.4), channel_id=1, source_target_pairs={{6,4},{14,12},{22,20},{30,28},{38,36},{46,44},{54,52},{62,60},{70,... | collective-permute-start | bytes 3145736 | tf_op jit(solution)/shard_map/ppermute | solution.py:250
  34.7 16.7 %collective-permute-start.3 = (f32[1024,256]{1,0:T(8,128)S(1)}, f32[1024,256]{1,0:T(8,128)S(1)}, u32[]{:S(2)}, u32[]{:S(2)}) collective-permute-start(f32[1024,256]{1,0:T(8,128)S(1)} %add_select_fusion.1.low), channel_id=1, source_target_pairs={{0,1},{2,3},{4,5},{6,7},{8,9},{10,11},{12,13},{14,15},{16,17},{18,... | collective-permute-start | bytes 3145736 | tf_op jit(solution)/shard_map/ppermute | solution.py:253
  40.2 11.2 %collective-permute-start.7 = (f32[1024,256]{1,0:T(8,128)S(1)}, f32[1024,256]{1,0:T(8,128)}, u32[]{:S(2)}, u32[]{:S(2)}) collective-permute-start(f32[1024,256]{1,0:T(8,128)S(1)} %add_select_fusion.high), channel_id=1, source_target_pairs={{0,1},{2,3},{4,5},{6,7},{8,9},{10,11},{12,13},{14,15},{16,17},{18,... | collective-permute-start | bytes 3145736 | tf_op jit(solution)/shard_map/ppermute | solution.py:254
  51.4 2.2 %copy-start = (bf16[2048,1024]{1,0:T(8,128)(2,1)S(1)}, bf16[2048,1024]{1,0:T(8,128)(2,1)}, u32[]{:S(2)}) copy-start(bf16[2048,1024]{1,0:T(8,128)(2,1)} %get-tuple-element.11.matrix_high) | copy-start | bytes 12582916
  53.6 2.2 %copy-start.1 = (bf16[2048,1024]{1,0:T(8,128)(2,1)S(1)}, bf16[2048,1024]{1,0:T(8,128)(2,1)}, u32[]{:S(2)}) copy-start(bf16[2048,1024]{1,0:T(8,128)(2,1)} %get-tuple-element.12.matrix_low) | copy-start | bytes 12582916
  62.4 1.0 copy-start.2
  63.4 1.0 copy-start.4
  64.4 40.5 %copy-start.3 = (bf16[2048,256]{1,0:T(8,128)(2,1)S(1)}, bf16[2048,256]{1,0:T(8,128)(2,1)}, u32[]{:S(2)}) copy-start(bf16[2048,256]{1,0:T(8,128)(2,1)} %copy-done.2) | copy-start | bytes 3145732
  64.4 40.5 %copy-start.5 = (bf16[2048,256]{1,0:T(8,128)(2,1)S(1)}, bf16[2048,256]{1,0:T(8,128)(2,1)}, u32[]{:S(2)}) copy-start(bf16[2048,256]{1,0:T(8,128)(2,1)} %copy-done.4) | copy-start | bytes 3145732
  86.7 18.2 %all-to-all-start.1 = ((f32[16,16,1280]{2,1,0:T(8,128)}), f32[16,16,1280]{2,1,0:T(8,128)S(1)}, u32[]{:S(2)}, u32[]{:S(2)}) async-start(f32[16,16,1280]{2,1,0:T(8,128)} %broadcast_in_dim.3), calls=%async_computation.1 | async-start | bytes 2621440 | tf_op jit(solution)/shard_map/all_to_all | solution.py:230

commit v2 on v1

--- a/solution.py
+++ b/solution.py
@@ -33,12 +33,16 @@
             pivot = jnp.broadcast_to(cols[j][gj][sj : sj + 1], (SUB, LANES))
             diagonal[gj] = jnp.where(row_id == sj, pivot, diagonal[gj])
             inverse = 1.0 / pivot
-            factor = {g: cols[j][g] * inverse for g in range(gj, groups)}
-            factor[gj] = jnp.where(row_id > sj, factor[gj], 0.0)
+            below = {g: cols[j][g] for g in range(gj, groups)}
+            below[gj] = jnp.where(row_id > sj, below[gj], 0.0)
+            factor = {g: below[g] * inverse for g in range(gj, groups)}
             for k in range(j + 1, p + panel):
                 row = jnp.broadcast_to(cols[k][gj][sj : sj + 1], (SUB, LANES))
                 for g in range(gj, groups):
-                    cols[k][g] = cols[k][g] - factor[g] * row
+                    if k == j + 1:
+                        cols[k][g] = cols[k][g] - (below[g] * row) * inverse
+                    else:
+                        cols[k][g] = cols[k][g] - factor[g] * row
             for h in range(2):
                 source = tiles[gj][h][sj : sj + 1]
                 if h == half:
@@ -105,24 +109,52 @@
     high[...], low[...] = split(matrix[...])
 
 
-def product_kernel(low, low_more, high, high_more, matrix_high, matrix_low, out, panel_high, panel_low):
-    half = low.shape[0]
-    cols = matrix_high.shape[1]
-    for first, more, start in ((low, low_more, 0), (high, high_more, half)):
+def pick_kernel(place, *refs):
+    sources, out, done = refs[:-2], refs[-2], refs[-1]
+    for z in range(4):
+
+        @pl.when(place[2] == z)
+        def _():
+            copies = []
+            begin = 0
+            for source in sources[2 * z : 2 * z + 2]:
+                step = source.shape[0] // 4
+                for i in range(4):
+                    copies.append(
+                        pltpu.make_async_copy(
+                            source.at[i * step : (i + 1) * step],
+                            out.at[begin + i * step : begin + (i + 1) * step],
+                            done.at[len(copies)],
+                        )
+                    )
+                begin += source.shape[0]
+            for copy in copies:
+                copy.start()
+            for copy in copies:
+                copy.wait()
+
+
+def product_kernel(place, panel_here, panel_sent, upper_pieces, upper_rest, lower_pieces, lower_rest, out, panel_high, panel_low):
+    half, cols = upper_pieces.shape
+    sent = place[3] == 1
+    for start, matrix_high, matrix_low in ((0, upper_pieces, upper_rest), (half, lower_pieces, lower_rest)):
         part = slice(start, start + half)
-        panel = first[...] + more[...]
-        panel_high[part], panel_low[part] = split(panel)
-        turned = panel.T
-        pieces = split(turned)
+        panel = jnp.where(sent, panel_sent[part], panel_here[part])
+        first, second = split(panel)
+        third = ((panel - first.astype(F32)) - second.astype(F32)).astype(jnp.bfloat16)
+        panel_high[part] = first
+        panel_low[part] = second
+        pieces = split(panel.T)
         for c in range(0, cols, PANEL):
             here = slice(c, c + PANEL)
-            value = split_dot(pieces, (matrix_high[part, here], matrix_low[part, here]))
+            value = split_dot(pieces, (matrix_high[:, here], matrix_low[:, here]))
             out[:, here] = value if start == 0 else out[:, here] + value
-        value = dot(turned, panel, NN, EXACT)
+        cross = dot(pieces[0], second, NN) + dot(pieces[0], third, NN)
+        value = dot(pieces[0], first, NN) + (dot(pieces[1], second, NN) + (cross + cross.T))
         out[:, cols:] = value if start == 0 else out[:, cols:] + value
 
 
-def finish_kernel(place, gathered, panel_high, panel_low, matrix, upper, out, work, inverse, coeff, coeff_low, held, arrived, left):
+def finish_kernel(place, gathered, panel_high, panel_low, matrix, upper, out, work, inverse, found, coeff, coeff_low, held, arrived, left):
     blocks = matrix.shape[0] // ROWS
     cols = matrix.shape[1]
     scale = float(matrix.shape[0] * (PANEL // upper.shape[0])) ** 0.5
@@ -147,12 +179,13 @@
     mine = pl.ds(pl.multiple_of(place[1] * height, height), height)
     for c in range(0, cols, PANEL):
         here = slice(c, c + PANEL)
-        work[...] = split_dot(lower, split(gathered[:, here]))
-        upper[:, here] = work[mine, :]
-        weights = split_dot(upward, split(work[...]))
+        part = split_dot(lower, split(gathered[:, here]))
+        found[:, here] = part
+        weights = split_dot(upward, split(part))
         if c == 0:
             weights = jnp.where(holds, -scale * turned, weights)
         coeff[:, here], coeff_low[:, here] = split(weights)
+    upper[...] = found[mine, :]
 
     for b in range(blocks):
         part = slice(b * ROWS, b * ROWS + ROWS)
@@ -175,30 +208,46 @@
 HBM = pl.BlockSpec(memory_space=pltpu.HBM)
 
 
-def prepare(matrix):
-    shape = jax.ShapeDtypeStruct(matrix.shape, jnp.bfloat16)
+def prepare(matrix, part=0, parts=1):
+    count = 2 * matrix.shape[0] // ROWS // parts
+    shape = jax.ShapeDtypeStruct((matrix.shape[0] // parts, matrix.shape[1]), jnp.bfloat16)
     block = pl.BlockSpec((ROWS // 2, matrix.shape[1]), lambda i: (i, 0))
     return pl.pallas_call(
         prepare_kernel,
-        grid=(2 * matrix.shape[0] // ROWS,),
+        grid=(count,),
         out_shape=(shape, shape),
-        in_specs=[block],
+        in_specs=[pl.BlockSpec((ROWS // 2, matrix.shape[1]), lambda i: (i + part * count, 0))],
         out_specs=(block, block),
-        cost_estimate=pl.CostEstimate(flops=3 * 10**9, bytes_accessed=16 << 20, transcendentals=0),
+        compiler_params=pltpu.CompilerParams(vmem_limit_bytes=12 << 20),
+        cost_estimate=pl.CostEstimate(flops=2 * 10**9, bytes_accessed=8 << 20, transcendentals=0),
     )(matrix)
 
 
-def products(low, low_more, high, high_more, pieces):
-    rows, cols = pieces[0].shape
+def pick(place, sources):
+    low, width = sources[0].shape
+    high = sources[1].shape[0]
+    return pl.pallas_call(
+        pick_kernel,
+        out_shape=jax.ShapeDtypeStruct((low + high, width), F32),
+        in_specs=[SMEM] + [HBM] * len(sources),
+        out_specs=VMEM,
+        scratch_shapes=[pltpu.SemaphoreType.DMA((8,))],
+        compiler_params=pltpu.CompilerParams(vmem_limit_bytes=8 << 20),
+        cost_estimate=pl.CostEstimate(flops=10**8, bytes_accessed=4 << 20, transcendentals=0),
+    )(place, *sources)
+
+
+def products(place, panel_here, panel_sent, pieces):
+    rows, cols = panel_here.shape[0], pieces[0].shape[1]
     narrow = jax.ShapeDtypeStruct((rows, PANEL), jnp.bfloat16)
     return pl.pallas_call(
         product_kernel,
         out_shape=(jax.ShapeDtypeStruct((PANEL, cols + PANEL), F32), narrow, narrow),
-        in_specs=[VMEM] * 6,
+        in_specs=[SMEM] + [VMEM] * 6,
         out_specs=[VMEM] * 3,
         compiler_params=pltpu.CompilerParams(vmem_limit_bytes=32 << 20),
         cost_estimate=pl.CostEstimate(flops=5 * 10**9, bytes_accessed=16 << 20, transcendentals=0),
-    )(low, low_more, high, high_more, *pieces)
+    )(place, panel_here, panel_sent, *pieces)
 
 
 def finish(place, gathered, panel_high, panel_low, matrix, height):
@@ -214,6 +263,7 @@
         scratch_shapes=[
             pltpu.VMEM((PANEL, PANEL), F32),
             pltpu.VMEM((PANEL, PANEL), F32),
+            pltpu.VMEM((PANEL, cols), F32),
             pltpu.VMEM((PANEL, cols), jnp.bfloat16),
             pltpu.VMEM((PANEL, cols), jnp.bfloat16),
             pltpu.VMEM(matrix.shape, F32),
@@ -237,25 +287,24 @@
 
 
 def shards(matrix):
-    holds = lax.axis_index(COL) == 0
-    half = matrix.shape[0] // 2
-    own_low, own_high = lax.optimization_barrier((matrix[:half, :PANEL], matrix[half:, :PANEL]))
-    swap = [(0, 1), (2, 3), (4, 5), (6, 7)]
-    low = lax.ppermute(own_low, COL, [(0, 2)])
-    high = lax.ppermute(own_high, COL, [(0, 6)])
-    low_too = lax.ppermute(own_low, COL, [(0, 6)])
-    high_too = lax.ppermute(own_high, COL, [(0, 2)])
-    pieces = prepare(matrix)
-    low_relay = lax.ppermute(low, COL, [(2, 4)])
-    high_relay = lax.ppermute(high, COL, [(6, 4)])
-    low = jnp.where(holds, own_low, low + low_too + low_relay)
-    high = jnp.where(holds, own_high, high + high_too + high_relay)
-    low_more = lax.ppermute(low, COL, swap)
-    high_more = lax.ppermute(high, COL, swap)
-    product, panel_high, panel_low = products(low, low_more, high, high_more, pieces)
+    col = lax.axis_index(COL)
+    place = jnp.stack([col == 0, lax.axis_index("row"), col // 2, col % 2]).astype(jnp.int32)
+    half = matrix.shape[0] * 35 // 64
+    own_low = lax.optimization_barrier(matrix[:half, :PANEL])
+    own_high = lax.optimization_barrier(matrix[half:, :PANEL])
+    first_low = lax.ppermute(own_low, COL, [(0, 2)])
+    first_high = lax.ppermute(own_high, COL, [(0, 6)])
+    second_low = lax.ppermute(own_low, COL, [(0, 6)])
+    second_high = lax.ppermute(own_high, COL, [(0, 2)])
+    pieces = prepare(matrix, 0, 2)
+    pieces += prepare(matrix, 1, 2)
+    relay_low = lax.ppermute(first_low, COL, [(2, 4)])
+    relay_high = lax.ppermute(first_high, COL, [(6, 4)])
+    here = pick(place, (own_low, own_high, first_low, second_high, relay_low, relay_high, second_low, first_high))
+    sent = lax.ppermute(here, COL, [(0, 1), (2, 3), (4, 5), (6, 7)])
+    product, panel_high, panel_low = products(place, here, sent, pieces)
     share = sum_at_owner(product, "row")
     gathered = from_everyone(share, "row").reshape(product.shape)
-    place = jnp.stack([holds.astype(jnp.int32), lax.axis_index("row").astype(jnp.int32)])
     upper, reduced = finish(place, gathered, panel_high, panel_low, matrix, share.shape[0])
     return (upper, reduced)
 

time: 121 us -> 118 us (0.975)
  blocking collectives: 21.1 us -> 49.8 us
  waiting for transfers between devices: 36.6 us -> 27 us
  local copies, waits for them, and re-layouts: 9.23 us -> 2.72 us
  Pallas kernels: 30.7 us -> 24.2 us
  starting transfers between devices: 17.3 us -> 11.2 us
  other arithmetic: 4.4 us -> 1.47 us
    all_to_all x0 -> x1, blocking collectives: none -> 22.6 us  [from_everyone(): return lax.all_to_all(copies, axis, 0, 0, tiled=True)]
    all_to_all x1 -> x0, waiting for transfers between devices: 14.2 us -> none  [from_everyone(): return lax.all_to_all(copies, axis, 0, 0, tiled=True)]
    unnamed x16 -> x2, local copies, waits for them, and re-layouts: 6.36 us -> 0.01 us
    all_to_all x1, blocking collectives: 21.1 us -> 27.2 us  [sum_at_owner(): return lax.all_to_all(tiles, axis, 0, 0, tiled=True).sum(0)]
    pallas_call x1 -> x3, Pallas kernels: 8.94 us -> 3.38 us  [the longest x1 2.12 us: pick(): pl.pallas_call(pick_kernel, out_shape=jax.ShapeDtypeStruct((low + high, w...]
    ppermute x8 -> x7, waiting for transfers between devices: 22.4 us -> 27 us  [the longest x1 12.7 us: shards(): second_high = lax.ppermute(own_high, COL, [(0, 2)])]
    select_n x2 -> x0, other arithmetic: 4.26 us -> none  [the longest x1 2.13 us: shards(): high = jnp.where(holds, own_high, high + high_too + high_relay)]
    all_to_all x1 -> x0, starting transfers between devices: 3.88 us -> none  [from_everyone(): return lax.all_to_all(copies, axis, 0, 0, tiled=True)]
  transfers between devices with their start and end apart: 9 -> 7, of which waited for: 4 -> 3; matrix products, arithmetic and copies ran while one was open for 4% -> 1% of each run, Pallas kernels for 7% -> 1%
where the time goes in v2:
time: 118 us; the launch traced here: 117 us
  blocking collectives  49.8 us (42%)
  waiting for transfers between devices  27 us (23%)
  Pallas kernels  24.2 us (21%)
  starting transfers between devices  11.2 us (9%)
  local copies, waits for them, and re-layouts  2.72 us (2%)
  other arithmetic  1.47 us (1%)
    all_to_all x1, blocking collectives, sum_at_owner(): return lax.all_to_all(tiles, axis, 0, 0, tiled=True).sum(0)  27.2 us
    all_to_all x1, blocking collectives, from_everyone(): return lax.all_to_all(copies, axis, 0, 0, tiled=True)  22.6 us
    pallas_call x1, Pallas kernels, finish(): pl.pallas_call(finish_kernel, out_shape=(jax.ShapeDtypeStruct((height, co...  15.6 us
    ppermute x1, waiting for transfers between devices, shards(): second_high = lax.ppermute(own_high, COL, [(0, 2)])  12.7 us
    ppermute x1, waiting for transfers between devices, shards(): first_low = lax.ppermute(own_low, COL, [(0, 2)])  11.9 us
    pallas_call x1, Pallas kernels, products(): pl.pallas_call(product_kernel, out_shape=(jax.ShapeDtypeStruct((PANEL, co...  5.22 us
  transfers between devices with their start and end apart: 7, of which 3 were waited for; matrix products, arithmetic and copies ran while one was open for 1% of the time, Pallas kernels for 1%

profile of v2, /device:TPU:32, one launch (start us, length us, event | category | flops | bytes accessed | tf_op | source)
XLA Modules:
  0.0 117.2 jit_solution(12561297009747493258)
XLA Ops:
  0.6 1.3 %slice.6.refs_0_ = f32[1120,256]{1,0:T(8,128)S(1)} slice(f32[2048,1024]{1,0:T(8,128)} %matrix.5), slice={[0:1120], [0:256]} | slice | bytes 2293760 | tf_op jit(solution)/shard_map/slice | solution.py:293
  2.0 1.3 %collective-permute-start = (f32[1120,256]{1,0:T(8,128)S(1)}, f32[1120,256]{1,0:T(8,128)S(1)}, u32[]{:S(2)}, u32[]{:S(2)}) collective-permute-start(f32[1120,256]{1,0:T(8,128)S(1)} %slice.6.refs_0_), channel_id=1, source_target_pairs={{0,2},{8,10},{16,18},{24,26},{32,34},{40,42},{48,50},{56,58},{64,6... | collective-permute-start | bytes 3440648 | tf_op jit(solution)/shard_map/ppermute | solution.py:295
  3.3 1.3 %slice.7.refs_1_ = f32[928,256]{1,0:T(8,128)S(1)} slice(f32[2048,1024]{1,0:T(8,128)} %matrix.5), slice={[1120:2048], [0:256]} | slice | bytes 1900544 | tf_op jit(solution)/shard_map/slice | solution.py:294
  4.5 1.6 %collective-permute-start.3 = (f32[928,256]{1,0:T(8,128)S(1)}, f32[928,256]{1,0:T(8,128)}, u32[]{:S(2)}, u32[]{:S(2)}) collective-permute-start(f32[928,256]{1,0:T(8,128)S(1)} %slice.7.refs_1_), channel_id=1, source_target_pairs={{0,6},{8,14},{16,22},{24,30},{32,38},{40,46},{48,54},{56,62},{64,7... | collective-permute-start | bytes 2850824 | tf_op jit(solution)/shard_map/ppermute | solution.py:296
  6.1 1.7 %collective-permute-start.5 = (f32[1120,256]{1,0:T(8,128)S(1)}, f32[1120,256]{1,0:T(8,128)}, u32[]{:S(2)}, u32[]{:S(2)}) collective-permute-start(f32[1120,256]{1,0:T(8,128)S(1)} %slice.6.refs_0_), channel_id=1, source_target_pairs={{0,6},{8,14},{16,22},{24,30},{32,38},{40,46},{48,54},{56,62},{64,7... | collective-permute-start | bytes 3440648 | tf_op jit(solution)/shard_map/ppermute | solution.py:297
  7.8 11.9 %collective-permute-done.refs_2_ = f32[1120,256]{1,0:T(8,128)S(1)} collective-permute-done((f32[1120,256]{1,0:T(8,128)S(1)}, f32[1120,256]{1,0:T(8,128)S(1)}, u32[]{:S(2)}, u32[]{:S(2)}) %collective-permute-start) | collective-permute-done | bytes 1146912 | tf_op jit(solution)/shard_map/ppermute | solution.py:295
  19.7 2.3 %collective-permute-start.2 = (f32[1120,256]{1,0:T(8,128)S(1)}, f32[1120,256]{1,0:T(8,128)}, u32[]{:S(2)}, u32[]{:S(2)}) collective-permute-start(f32[1120,256]{1,0:T(8,128)S(1)} %collective-permute-done.refs_2_), channel_id=1, source_target_pairs={{2,4},{10,12},{18,20},{26,28},{34,36},{42,44},{50,52},{58,60},{66,... | collective-permute-start | bytes 3440648 | tf_op jit(solution)/shard_map/ppermute | solution.py:301
  22.0 1.3 %collective-permute-start.1 = (f32[928,256]{1,0:T(8,128)S(1)}, f32[928,256]{1,0:T(8,128)}, u32[]{:S(2)}, u32[]{:S(2)}) collective-permute-start(f32[928,256]{1,0:T(8,128)S(1)} %slice.7.refs_1_), channel_id=1, source_target_pairs={{0,2},{8,10},{16,18},{24,26},{32,34},{40,42},{48,50},{56,58},{64,6... | collective-permute-start | bytes 2850824 | tf_op jit(solution)/shard_map/ppermute | solution.py:298
  23.3 0.0 collective-permute-done.3.refs_7_
  23.3 1.6 %collective-permute-start.4 = (f32[928,256]{1,0:T(8,128)}, f32[928,256]{1,0:T(8,128)}, u32[]{:S(2)}, u32[]{:S(2)}) collective-permute-start(f32[928,256]{1,0:T(8,128)} %collective-permute-done.3.refs_7_), channel_id=1, source_target_pairs={{6,4},{14,12},{22,20},{30,28},{38,36},{46,44},{54,52},{62,60},{70,... | collective-permute-start | bytes 2850824 | tf_op jit(solution)/shard_map/ppermute | solution.py:302
  24.9 0.1 pad_add_fusion.place
  25.0 0.0 copy-start
  25.0 12.7 %collective-permute-done.1.refs_3_ = f32[928,256]{1,0:T(8,128)} collective-permute-done((f32[928,256]{1,0:T(8,128)S(1)}, f32[928,256]{1,0:T(8,128)}, u32[]{:S(2)}, u32[]{:S(2)}) %collective-permute-start.1) | collective-permute-done | bytes 950304 | tf_op jit(solution)/shard_map/ppermute | solution.py:298
  37.8 0.0 collective-permute-done.5.refs_6_
  37.8 0.0 collective-permute-done.4.refs_5_
  37.8 0.0 collective-permute-done.2.refs_4_
  37.8 2.1 %shard_map.30.panel_here = f32[2048,256]{1,0:T(8,128)S(1)} custom-call(s32[4]{0:T(128)S(1)} %pad_add_fusion.place, f32[1120,256]{1,0:T(8,128)S(1)} %slice.6.refs_0_, f32[928,256]{1,0:T(8,128)S(1)} %slice.7.refs_1_, f32[1120,256]{1,0:T(8,128)S(1)} %collective-permute-done.refs_2_, f32[928,256]{1,0:T(8,128)} %collective-permute-done.1.refs_3_, ...), custom_call_target="tpu_custom_call" | custom-call | flops 100000000 | bytes 4194304 | tf_op jit(solution)/shard_map/pallas_call | solution.py:229
  39.9 1.4 %collective-permute-start.6 = (f32[2048,256]{1,0:T(8,128)S(1)}, f32[2048,256]{1,0:T(8,128)S(1)}, u32[]{:S(2)}, u32[]{:S(2)}) collective-permute-start(f32[2048,256]{1,0:T(8,128)S(1)} %shard_map.30.panel_here), channel_id=1, source_target_pairs={{0,1},{2,3},{4,5},{6,7},{8,9},{10,11},{12,13},{14,15},{16,17},{18,... | collective-permute-start | bytes 6291464 | tf_op jit(solution)/shard_map/ppermute | solution.py:304
  41.3 0.0 copy-done
  41.3 0.6 shard_map.31
  42.0 0.6 shard_map.32
  42.6 2.4 %collective-permute-done.6.panel_sent = f32[2048,256]{1,0:T(8,128)S(1)} collective-permute-done((f32[2048,256]{1,0:T(8,128)S(1)}, f32[2048,256]{1,0:T(8,128)S(1)}, u32[]{:S(2)}, u32[]{:S(2)}) %collective-permute-start.6) | collective-permute-done | bytes 2097184 | tf_op jit(solution)/shard_map/ppermute | solution.py:304
  45.0 5.2 %shard_map.33 = (f32[256,1280]{1,0:T(8,128)S(1)}, bf16[2048,256]{1,0:T(8,128)(2,1)S(1)}, bf16[2048,256]{1,0:T(8,128)(2,1)S(1)}) custom-call(s32[4]{0:T(128)S(1)} %pad_add_fusion.place, f32[2048,256]{1,0:T(8,128)S(1)} %shard_map.30.panel_here, f32[2048,256]{1,0:T(8,128)S(1)} %collective-permute-done.6.panel_sent, ...), custom_call_target="tpu_custom_call" | custom-call | flops 5000000000 | bytes 16777216 | tf_op jit(solution)/shard_map/pallas_call | solution.py:243
  50.2 27.2 %all_to_all.10 = f32[16,16,1280]{2,1,0:T(8,128)} all-to-all(f32[16,16,1280]{2,1,0:T(8,128)S(1)} %bitcast.6), channel_id=1, replica_groups=mesh['row'=16,'z'=4,'c'=2] {'row'}, dimensions={0} | all-to-all | bytes 2621440 | tf_op jit(solution)/shard_map/all_to_all | solution.py:286
  77.4 1.4 %reduce_sum.9 = f32[16,1280]{1,0:T(8,128)S(1)} reduce(f32[16,16,1280]{2,1,0:T(8,128)} %all_to_all.10, f32[]{:T(128)} %constant.39.clone.1), dimensions={0}, to_apply=%region_0.1 | reduce | flops 307200 | bytes 1392644 | tf_op jit(solution)/shard_map/reduce_sum | solution.py:286
  78.8 0.1 broadcast_in_dim.3
  78.9 22.6 %all_to_all.11 = f32[16,16,1280]{2,1,0:T(8,128)S(1)} all-to-all(f32[16,16,1280]{2,1,0:T(8,128)S(1)} %broadcast_in_dim.3), channel_id=1, replica_groups=mesh['row'=16,'z'=4,'c'=2] {'row'}, dimensions={0} | all-to-all | bytes 2621440 | tf_op jit(solution)/shard_map/all_to_all | solution.py:280
  101.5 15.6 %shard_map.34 = (f32[16,1024]{1,0:T(8,128)}, f32[2048,1024]{1,0:T(8,128)}) custom-call(s32[4]{0:T(128)S(1)} %pad_add_fusion.place, f32[256,1280]{1,0:T(8,128)S(1)} %bitcast.7, bf16[2048,256]{1,0:T(8,128)(2,1)S(1)} %get-tuple-element.14.panel_high, bf16[2048,256]{1,0:T(8,128)(2,1)S(1)} %get-tuple-element.15.panel_low, f32[2048,1024]{1,0:T(8,128)} %matrix.5), custom_call_target="tpu_custom_call" | custom-call | flops 8000000000 | bytes 25165824 | tf_op jit(solution)/shard_map/pallas_call | solution.py:255
Async XLA Ops:
  2.0 17.7 %collective-permute-start = (f32[1120,256]{1,0:T(8,128)S(1)}, f32[1120,256]{1,0:T(8,128)S(1)}, u32[]{:S(2)}, u32[]{:S(2)}) collective-permute-start(f32[1120,256]{1,0:T(8,128)S(1)} %slice.6.refs_0_), channel_id=1, source_target_pairs={{0,2},{8,10},{16,18},{24,26},{32,34},{40,42},{48,50},{56,58},{64,6... | collective-permute-start | bytes 3440648 | tf_op jit(solution)/shard_map/ppermute | solution.py:295
  4.5 18.8 %collective-permute-start.3 = (f32[928,256]{1,0:T(8,128)S(1)}, f32[928,256]{1,0:T(8,128)}, u32[]{:S(2)}, u32[]{:S(2)}) collective-permute-start(f32[928,256]{1,0:T(8,128)S(1)} %slice.7.refs_1_), channel_id=1, source_target_pairs={{0,6},{8,14},{16,22},{24,30},{32,38},{40,46},{48,54},{56,62},{64,7... | collective-permute-start | bytes 2850824 | tf_op jit(solution)/shard_map/ppermute | solution.py:296
  6.1 31.6 %collective-permute-start.5 = (f32[1120,256]{1,0:T(8,128)S(1)}, f32[1120,256]{1,0:T(8,128)}, u32[]{:S(2)}, u32[]{:S(2)}) collective-permute-start(f32[1120,256]{1,0:T(8,128)S(1)} %slice.6.refs_0_), channel_id=1, source_target_pairs={{0,6},{8,14},{16,22},{24,30},{32,38},{40,46},{48,54},{56,62},{64,7... | collective-permute-start | bytes 3440648 | tf_op jit(solution)/shard_map/ppermute | solution.py:297
  19.7 18.0 %collective-permute-start.2 = (f32[1120,256]{1,0:T(8,128)S(1)}, f32[1120,256]{1,0:T(8,128)}, u32[]{:S(2)}, u32[]{:S(2)}) collective-permute-start(f32[1120,256]{1,0:T(8,128)S(1)} %collective-permute-done.refs_2_), channel_id=1, source_target_pairs={{2,4},{10,12},{18,20},{26,28},{34,36},{42,44},{50,52},{58,60},{66,... | collective-permute-start | bytes 3440648 | tf_op jit(solution)/shard_map/ppermute | solution.py:301
  22.0 15.7 %collective-permute-start.1 = (f32[928,256]{1,0:T(8,128)S(1)}, f32[928,256]{1,0:T(8,128)}, u32[]{:S(2)}, u32[]{:S(2)}) collective-permute-start(f32[928,256]{1,0:T(8,128)S(1)} %slice.7.refs_1_), channel_id=1, source_target_pairs={{0,2},{8,10},{16,18},{24,26},{32,34},{40,42},{48,50},{56,58},{64,6... | collective-permute-start | bytes 2850824 | tf_op jit(solution)/shard_map/ppermute | solution.py:298
  23.3 14.4 %collective-permute-start.4 = (f32[928,256]{1,0:T(8,128)}, f32[928,256]{1,0:T(8,128)}, u32[]{:S(2)}, u32[]{:S(2)}) collective-permute-start(f32[928,256]{1,0:T(8,128)} %collective-permute-done.3.refs_7_), channel_id=1, source_target_pairs={{6,4},{14,12},{22,20},{30,28},{38,36},{46,44},{54,52},{62,60},{70,... | collective-permute-start | bytes 2850824 | tf_op jit(solution)/shard_map/ppermute | solution.py:302
  25.0 16.3 %copy-start = (f32[2048,1024]{1,0:T(8,128)S(1)}, f32[2048,1024]{1,0:T(8,128)}, u32[]{:S(2)}) copy-start(f32[2048,1024]{1,0:T(8,128)} %matrix.5) | copy-start | bytes 25165828
  39.9 5.1 %collective-permute-start.6 = (f32[2048,256]{1,0:T(8,128)S(1)}, f32[2048,256]{1,0:T(8,128)S(1)}, u32[]{:S(2)}, u32[]{:S(2)}) collective-permute-start(f32[2048,256]{1,0:T(8,128)S(1)} %shard_map.30.panel_here), channel_id=1, source_target_pairs={{0,1},{2,3},{4,5},{6,7},{8,9},{10,11},{12,13},{14,15},{16,17},{18,... | collective-permute-start | bytes 6291464 | tf_op jit(solution)/shard_map/ppermute | solution.py:304

commit v3 on v2

--- a/solution.py
+++ b/solution.py
@@ -275,15 +275,30 @@
     )(place, gathered, panel_high, panel_low, matrix)
 
 
-def from_everyone(shard, axis):
-    copies = jnp.broadcast_to(shard, (lax.axis_size(axis), *shard.shape))
-    return lax.all_to_all(copies, axis, 0, 0, tiled=True)
-
-
-def sum_at_owner(shard, axis):
-    count = lax.axis_size(axis)
-    tiles = shard.reshape(count, shard.shape[0] // count, shard.shape[1])
-    return lax.all_to_all(tiles, axis, 0, 0, tiled=True).sum(0)
+def total_kernel(tiles, out):
+    total = tiles[0]
+    for i in range(1, tiles.shape[0]):
+        total = total + tiles[i]
+    for i in range(out.shape[0]):
+        out[i] = total
+
+
+def exchange(tiles):
+    return lax.all_to_all(tiles, "row", 0, 0, tiled=True)
+
+
+def sum_everywhere(value):
+    count = lax.axis_size("row")
+    tiles = exchange(value.reshape(count, value.shape[0] // count, value.shape[1]))
+    copies = pl.pallas_call(
+        total_kernel,
+        out_shape=jax.ShapeDtypeStruct(tiles.shape, F32),
+        in_specs=[VMEM],
+        out_specs=VMEM,
+        compiler_params=pltpu.CompilerParams(vmem_limit_bytes=8 << 20),
+        cost_estimate=pl.CostEstimate(flops=10**7, bytes_accessed=3 << 20, transcendentals=0),
+    )(tiles)
+    return exchange(copies).reshape(value.shape)
 
 
 def shards(matrix):
@@ -303,9 +318,9 @@
     here = pick(place, (own_low, own_high, first_low, second_high, relay_low, relay_high, second_low, first_high))
     sent = lax.ppermute(here, COL, [(0, 1), (2, 3), (4, 5), (6, 7)])
     product, panel_high, panel_low = products(place, here, sent, pieces)
-    share = sum_at_owner(product, "row")
-    gathered = from_everyone(share, "row").reshape(product.shape)
-    upper, reduced = finish(place, gathered, panel_high, panel_low, matrix, share.shape[0])
+    gathered = sum_everywhere(product)
+    height = PANEL // lax.axis_size("row")
+    upper, reduced = finish(place, gathered, panel_high, panel_low, matrix, height)
     return (upper, reduced)
 
 

time: 118 us -> 116 us (0.983)
  other arithmetic: 1.47 us -> 0.08 us
    reduce_sum x1 -> x0, other arithmetic: 1.39 us -> none  [sum_at_owner(): return lax.all_to_all(tiles, axis, 0, 0, tiled=True).sum(0)]
where the time goes in v3:
time: 116 us
  blocking collectives  49.7 us (43%)
  waiting for transfers between devices  27 us (23%)
  Pallas kernels  24.4 us (21%)
  starting transfers between devices  11.2 us (10%)
  local copies, waits for them, and re-layouts  2.6 us (2%)
    all_to_all x2, blocking collectives, exchange(): return lax.all_to_all(tiles, 'row', 0, 0, tiled=True)  49.7 us
    pallas_call x1, Pallas kernels, finish(): pl.pallas_call(finish_kernel, out_shape=(jax.ShapeDtypeStruct((height, co...  15.6 us
    ppermute x1, waiting for transfers between devices, shards(): second_high = lax.ppermute(own_high, COL, [(0, 2)])  12.7 us
    ppermute x1, waiting for transfers between devices, shards(): first_low = lax.ppermute(own_low, COL, [(0, 2)])  12 us
    pallas_call x1, Pallas kernels, products(): pl.pallas_call(product_kernel, out_shape=(jax.ShapeDtypeStruct((PANEL, co...  5.28 us
  transfers between devices with their start and end apart: 7, of which 3 were waited for; matrix products, arithmetic and copies ran while one was open for 1% of the time, Pallas kernels for 1%

profile of v3, /device:TPU:32, one launch (start us, length us, event | category | flops | bytes accessed | tf_op | source)
XLA Modules:
  0.0 115.9 jit_solution(2272904934348384683)
XLA Ops:
  0.6 1.3 %slice.6.refs_0_ = f32[1120,256]{1,0:T(8,128)S(1)} slice(f32[2048,1024]{1,0:T(8,128)} %matrix.5), slice={[0:1120], [0:256]} | slice | bytes 2293760 | tf_op jit(solution)/shard_map/slice | solution.py:308
  2.0 1.3 %collective-permute-start = (f32[1120,256]{1,0:T(8,128)S(1)}, f32[1120,256]{1,0:T(8,128)}, u32[]{:S(2)}, u32[]{:S(2)}) collective-permute-start(f32[1120,256]{1,0:T(8,128)S(1)} %slice.6.refs_0_), channel_id=1, source_target_pairs={{0,2},{8,10},{16,18},{24,26},{32,34},{40,42},{48,50},{56,58},{64,6... | collective-permute-start | bytes 3440648 | tf_op jit(solution)/shard_map/ppermute | solution.py:310
  3.3 1.3 %slice.7.refs_1_ = f32[928,256]{1,0:T(8,128)S(1)} slice(f32[2048,1024]{1,0:T(8,128)} %matrix.5), slice={[1120:2048], [0:256]} | slice | bytes 1900544 | tf_op jit(solution)/shard_map/slice | solution.py:309
  4.5 1.6 %collective-permute-start.3 = (f32[928,256]{1,0:T(8,128)S(1)}, f32[928,256]{1,0:T(8,128)}, u32[]{:S(2)}, u32[]{:S(2)}) collective-permute-start(f32[928,256]{1,0:T(8,128)S(1)} %slice.7.refs_1_), channel_id=1, source_target_pairs={{0,6},{8,14},{16,22},{24,30},{32,38},{40,46},{48,54},{56,62},{64,7... | collective-permute-start | bytes 2850824 | tf_op jit(solution)/shard_map/ppermute | solution.py:311
  6.2 1.7 %collective-permute-start.5 = (f32[1120,256]{1,0:T(8,128)S(1)}, f32[1120,256]{1,0:T(8,128)}, u32[]{:S(2)}, u32[]{:S(2)}) collective-permute-start(f32[1120,256]{1,0:T(8,128)S(1)} %slice.6.refs_0_), channel_id=1, source_target_pairs={{0,6},{8,14},{16,22},{24,30},{32,38},{40,46},{48,54},{56,62},{64,7... | collective-permute-start | bytes 3440648 | tf_op jit(solution)/shard_map/ppermute | solution.py:312
  7.8 12.0 %collective-permute-done.refs_2_ = f32[1120,256]{1,0:T(8,128)} collective-permute-done((f32[1120,256]{1,0:T(8,128)S(1)}, f32[1120,256]{1,0:T(8,128)}, u32[]{:S(2)}, u32[]{:S(2)}) %collective-permute-start) | collective-permute-done | bytes 1146912 | tf_op jit(solution)/shard_map/ppermute | solution.py:310
  19.8 2.3 %collective-permute-start.2 = (f32[1120,256]{1,0:T(8,128)}, f32[1120,256]{1,0:T(8,128)}, u32[]{:S(2)}, u32[]{:S(2)}) collective-permute-start(f32[1120,256]{1,0:T(8,128)} %collective-permute-done.refs_2_), channel_id=1, source_target_pairs={{2,4},{10,12},{18,20},{26,28},{34,36},{42,44},{50,52},{58,60},{66,... | collective-permute-start | bytes 3440648 | tf_op jit(solution)/shard_map/ppermute | solution.py:316
  22.1 1.3 %collective-permute-start.1 = (f32[928,256]{1,0:T(8,128)S(1)}, f32[928,256]{1,0:T(8,128)}, u32[]{:S(2)}, u32[]{:S(2)}) collective-permute-start(f32[928,256]{1,0:T(8,128)S(1)} %slice.7.refs_1_), channel_id=1, source_target_pairs={{0,2},{8,10},{16,18},{24,26},{32,34},{40,42},{48,50},{56,58},{64,6... | collective-permute-start | bytes 2850824 | tf_op jit(solution)/shard_map/ppermute | solution.py:313
  23.4 0.0 collective-permute-done.3.refs_7_
  23.4 1.6 %collective-permute-start.4 = (f32[928,256]{1,0:T(8,128)}, f32[928,256]{1,0:T(8,128)}, u32[]{:S(2)}, u32[]{:S(2)}) collective-permute-start(f32[928,256]{1,0:T(8,128)} %collective-permute-done.3.refs_7_), channel_id=1, source_target_pairs={{6,4},{14,12},{22,20},{30,28},{38,36},{46,44},{54,52},{62,60},{70,... | collective-permute-start | bytes 2850824 | tf_op jit(solution)/shard_map/ppermute | solution.py:317
  25.0 0.1 pad_add_fusion.place
  25.1 0.0 copy-start
  25.1 12.7 %collective-permute-done.1.refs_3_ = f32[928,256]{1,0:T(8,128)} collective-permute-done((f32[928,256]{1,0:T(8,128)S(1)}, f32[928,256]{1,0:T(8,128)}, u32[]{:S(2)}, u32[]{:S(2)}) %collective-permute-start.1) | collective-permute-done | bytes 950304 | tf_op jit(solution)/shard_map/ppermute | solution.py:313
  37.8 0.0 collective-permute-done.5.refs_6_
  37.9 0.0 collective-permute-done.4.refs_5_
  37.9 0.0 collective-permute-done.2.refs_4_
  37.9 2.1 %shard_map.30.panel_here = f32[2048,256]{1,0:T(8,128)S(1)} custom-call(s32[4]{0:T(128)S(1)} %pad_add_fusion.place, f32[1120,256]{1,0:T(8,128)S(1)} %slice.6.refs_0_, f32[928,256]{1,0:T(8,128)S(1)} %slice.7.refs_1_, f32[1120,256]{1,0:T(8,128)} %collective-permute-done.refs_2_, f32[928,256]{1,0:T(8,128)} %collective-permute-done.1.refs_3_, ...), custom_call_target="tpu_custom_call" | custom-call | flops 100000000 | bytes 4194304 | tf_op jit(solution)/shard_map/pallas_call | solution.py:229
  40.0 1.4 %collective-permute-start.6 = (f32[2048,256]{1,0:T(8,128)S(1)}, f32[2048,256]{1,0:T(8,128)S(1)}, u32[]{:S(2)}, u32[]{:S(2)}) collective-permute-start(f32[2048,256]{1,0:T(8,128)S(1)} %shard_map.30.panel_here), channel_id=1, source_target_pairs={{0,1},{2,3},{4,5},{6,7},{8,9},{10,11},{12,13},{14,15},{16,17},{18,... | collective-permute-start | bytes 6291464 | tf_op jit(solution)/shard_map/ppermute | solution.py:319
  41.4 0.0 copy-done
  41.4 0.7 shard_map.31
  42.1 0.7 shard_map.32
  42.8 2.3 %collective-permute-done.6.panel_sent = f32[2048,256]{1,0:T(8,128)S(1)} collective-permute-done((f32[2048,256]{1,0:T(8,128)S(1)}, f32[2048,256]{1,0:T(8,128)S(1)}, u32[]{:S(2)}, u32[]{:S(2)}) %collective-permute-start.6) | collective-permute-done | bytes 2097184 | tf_op jit(solution)/shard_map/ppermute | solution.py:319
  45.1 5.3 %shard_map.33 = (f32[256,1280]{1,0:T(8,128)S(1)}, bf16[2048,256]{1,0:T(8,128)(2,1)S(1)}, bf16[2048,256]{1,0:T(8,128)(2,1)S(1)}) custom-call(s32[4]{0:T(128)S(1)} %pad_add_fusion.place, f32[2048,256]{1,0:T(8,128)S(1)} %shard_map.30.panel_here, f32[2048,256]{1,0:T(8,128)S(1)} %collective-permute-done.6.panel_sent, ...), custom_call_target="tpu_custom_call" | custom-call | flops 5000000000 | bytes 16777216 | tf_op jit(solution)/shard_map/pallas_call | solution.py:243
  50.3 27.1 %all_to_all.10.tiles = f32[16,16,1280]{2,1,0:T(8,128)S(1)} all-to-all(f32[16,16,1280]{2,1,0:T(8,128)S(1)} %bitcast.6), channel_id=1, replica_groups=mesh['row'=16,'z'=4,'c'=2] {'row'}, dimensions={0} | all-to-all | bytes 2621440 | tf_op jit(solution)/shard_map/all_to_all | solution.py:287
  77.5 0.1 shard_map.34
  77.6 22.6 %all_to_all.11 = f32[16,16,1280]{2,1,0:T(8,128)S(1)} all-to-all(f32[16,16,1280]{2,1,0:T(8,128)S(1)} %shard_map.34), channel_id=1, replica_groups=mesh['row'=16,'z'=4,'c'=2] {'row'}, dimensions={0} | all-to-all | bytes 2621440 | tf_op jit(solution)/shard_map/all_to_all | solution.py:287
  100.2 15.6 %shard_map.35 = (f32[16,1024]{1,0:T(8,128)}, f32[2048,1024]{1,0:T(8,128)}) custom-call(s32[4]{0:T(128)S(1)} %pad_add_fusion.place, f32[256,1280]{1,0:T(8,128)S(1)} %bitcast.7, bf16[2048,256]{1,0:T(8,128)(2,1)S(1)} %get-tuple-element.14.panel_high, bf16[2048,256]{1,0:T(8,128)(2,1)S(1)} %get-tuple-element.15.panel_low, f32[2048,1024]{1,0:T(8,128)} %matrix.5), custom_call_target="tpu_custom_call" | custom-call | flops 8000000000 | bytes 25165824 | tf_op jit(solution)/shard_map/pallas_call | solution.py:255
Async XLA Ops:
  2.0 17.9 %collective-permute-start = (f32[1120,256]{1,0:T(8,128)S(1)}, f32[1120,256]{1,0:T(8,128)}, u32[]{:S(2)}, u32[]{:S(2)}) collective-permute-start(f32[1120,256]{1,0:T(8,128)S(1)} %slice.6.refs_0_), channel_id=1, source_target_pairs={{0,2},{8,10},{16,18},{24,26},{32,34},{40,42},{48,50},{56,58},{64,6... | collective-permute-start | bytes 3440648 | tf_op jit(solution)/shard_map/ppermute | solution.py:310
  4.5 18.9 %collective-permute-start.3 = (f32[928,256]{1,0:T(8,128)S(1)}, f32[928,256]{1,0:T(8,128)}, u32[]{:S(2)}, u32[]{:S(2)}) collective-permute-start(f32[928,256]{1,0:T(8,128)S(1)} %slice.7.refs_1_), channel_id=1, source_target_pairs={{0,6},{8,14},{16,22},{24,30},{32,38},{40,46},{48,54},{56,62},{64,7... | collective-permute-start | bytes 2850824 | tf_op jit(solution)/shard_map/ppermute | solution.py:311
  6.2 31.7 %collective-permute-start.5 = (f32[1120,256]{1,0:T(8,128)S(1)}, f32[1120,256]{1,0:T(8,128)}, u32[]{:S(2)}, u32[]{:S(2)}) collective-permute-start(f32[1120,256]{1,0:T(8,128)S(1)} %slice.6.refs_0_), channel_id=1, source_target_pairs={{0,6},{8,14},{16,22},{24,30},{32,38},{40,46},{48,54},{56,62},{64,7... | collective-permute-start | bytes 3440648 | tf_op jit(solution)/shard_map/ppermute | solution.py:312
  19.8 18.0 %collective-permute-start.2 = (f32[1120,256]{1,0:T(8,128)}, f32[1120,256]{1,0:T(8,128)}, u32[]{:S(2)}, u32[]{:S(2)}) collective-permute-start(f32[1120,256]{1,0:T(8,128)} %collective-permute-done.refs_2_), channel_id=1, source_target_pairs={{2,4},{10,12},{18,20},{26,28},{34,36},{42,44},{50,52},{58,60},{66,... | collective-permute-start | bytes 3440648 | tf_op jit(solution)/shard_map/ppermute | solution.py:316
  22.1 15.7 %collective-permute-start.1 = (f32[928,256]{1,0:T(8,128)S(1)}, f32[928,256]{1,0:T(8,128)}, u32[]{:S(2)}, u32[]{:S(2)}) collective-permute-start(f32[928,256]{1,0:T(8,128)S(1)} %slice.7.refs_1_), channel_id=1, source_target_pairs={{0,2},{8,10},{16,18},{24,26},{32,34},{40,42},{48,50},{56,58},{64,6... | collective-permute-start | bytes 2850824 | tf_op jit(solution)/shard_map/ppermute | solution.py:313
  23.4 14.4 %collective-permute-start.4 = (f32[928,256]{1,0:T(8,128)}, f32[928,256]{1,0:T(8,128)}, u32[]{:S(2)}, u32[]{:S(2)}) collective-permute-start(f32[928,256]{1,0:T(8,128)} %collective-permute-done.3.refs_7_), channel_id=1, source_target_pairs={{6,4},{14,12},{22,20},{30,28},{38,36},{46,44},{54,52},{62,60},{70,... | collective-permute-start | bytes 2850824 | tf_op jit(solution)/shard_map/ppermute | solution.py:317
  25.1 16.3 %copy-start = (f32[2048,1024]{1,0:T(8,128)S(1)}, f32[2048,1024]{1,0:T(8,128)}, u32[]{:S(2)}) copy-start(f32[2048,1024]{1,0:T(8,128)} %matrix.5) | copy-start | bytes 25165828
  40.0 5.1 %collective-permute-start.6 = (f32[2048,256]{1,0:T(8,128)S(1)}, f32[2048,256]{1,0:T(8,128)S(1)}, u32[]{:S(2)}, u32[]{:S(2)}) collective-permute-start(f32[2048,256]{1,0:T(8,128)S(1)} %shard_map.30.panel_here), channel_id=1, source_target_pairs={{0,1},{2,3},{4,5},{6,7},{8,9},{10,11},{12,13},{14,15},{16,17},{18,... | collective-permute-start | bytes 6291464 | tf_op jit(solution)/shard_map/ppermute | solution.py:319

commit v4 on v3

--- a/solution.py
+++ b/solution.py
@@ -65,7 +65,7 @@
     return out
 
 
-def factor(work, inverse):
+def factor(work, inverse, visit):
     n = work.shape[0]
     col_id = lax.broadcasted_iota(jnp.int32, (BLOCK, n), 1)
     for start in range(0, n, BLOCK):
@@ -77,6 +77,7 @@
         rows = jnp.concatenate([jnp.concatenate(t, axis=1) for t in done], axis=0)
         inverse[start : start + BLOCK, :] = jnp.where(col_id < start + BLOCK, rows, 0.0)
         after = start + BLOCK
+        visit(start, after)
         for lo, hi in ((after, after + BLOCK), (after + BLOCK, n)):
             if lo >= n or lo >= hi:
                 continue
@@ -154,7 +155,7 @@
         out[:, cols:] = value if start == 0 else out[:, cols:] + value
 
 
-def finish_kernel(place, gathered, panel_high, panel_low, matrix, upper, out, work, inverse, found, coeff, coeff_low, held, arrived, left):
+def finish_kernel(place, gathered, panel_high, panel_low, matrix, upper, out, work, inverse, found, first, second, coeff, coeff_low, held, arrived, left):
     blocks = matrix.shape[0] // ROWS
     cols = matrix.shape[1]
     scale = float(matrix.shape[0] * (PANEL // upper.shape[0])) ** 0.5
@@ -171,17 +172,21 @@
         fetch(b).start()
     holds = place[0] == 1
     work[...] = gathered[:, cols:]
-    factor(work, inverse)
-    lower = split(inverse[...])
+    first[...], second[...] = split(gathered[:, :cols])
+
+    def visit(start, after):
+        depth = -(-after // LANES) * LANES
+        rows = split(inverse[start:after, :depth])
+        found[start:after, :] = split_dot(rows, (first[:depth, :], second[:depth, :]))
+
+    factor(work, inverse, visit)
     turned = inverse[...].T
     upward = split(turned)
     height = upper.shape[0]
     mine = pl.ds(pl.multiple_of(place[1] * height, height), height)
     for c in range(0, cols, PANEL):
         here = slice(c, c + PANEL)
-        part = split_dot(lower, split(gathered[:, here]))
-        found[:, here] = part
-        weights = split_dot(upward, split(part))
+        weights = split_dot(upward, split(found[:, here]))
         if c == 0:
             weights = jnp.where(holds, -scale * turned, weights)
         coeff[:, here], coeff_low[:, here] = split(weights)
@@ -264,6 +269,8 @@
             pltpu.VMEM((PANEL, PANEL), F32),
             pltpu.VMEM((PANEL, PANEL), F32),
             pltpu.VMEM((PANEL, cols), F32),
+            pltpu.VMEM((PANEL, cols), jnp.bfloat16),
+            pltpu.VMEM((PANEL, cols), jnp.bfloat16),
             pltpu.VMEM((PANEL, cols), jnp.bfloat16),
             pltpu.VMEM((PANEL, cols), jnp.bfloat16),
             pltpu.VMEM(matrix.shape, F32),

time: 116 us -> 116 us (level)
  no operation moved by 1% of the time
where the time goes in v4:
time: 116 us
  blocking collectives  49.7 us (43%)
  waiting for transfers between devices  27 us (23%)
  Pallas kernels  24.2 us (21%)
  starting transfers between devices  11.2 us (10%)
  local copies, waits for them, and re-layouts  2.6 us (2%)
    all_to_all x2, blocking collectives, exchange(): return lax.all_to_all(tiles, 'row', 0, 0, tiled=True)  49.7 us
    pallas_call x1, Pallas kernels, finish(): pl.pallas_call(finish_kernel, out_shape=(jax.ShapeDtypeStruct((height, co...  15.3 us
    ppermute x1, waiting for transfers between devices, shards(): second_high = lax.ppermute(own_high, COL, [(0, 2)])  12.7 us
    ppermute x1, waiting for transfers between devices, shards(): first_low = lax.ppermute(own_low, COL, [(0, 2)])  12 us
    pallas_call x1, Pallas kernels, products(): pl.pallas_call(product_kernel, out_shape=(jax.ShapeDtypeStruct((PANEL, co...  5.28 us
  transfers between devices with their start and end apart: 7, of which 3 were waited for; matrix products, arithmetic and copies ran while one was open for 1% of the time, Pallas kernels for 1%

profile of v4, /device:TPU:32, one launch (start us, length us, event | category | flops | bytes accessed | tf_op | source)
XLA Modules:
  0.0 115.6 jit_solution(13102077292641367705)
XLA Ops:
  0.6 1.3 %slice.6.refs_0_ = f32[1120,256]{1,0:T(8,128)S(1)} slice(f32[2048,1024]{1,0:T(8,128)} %matrix.5), slice={[0:1120], [0:256]} | slice | bytes 2293760 | tf_op jit(solution)/shard_map/slice | solution.py:315
  2.0 1.3 %collective-permute-start = (f32[1120,256]{1,0:T(8,128)S(1)}, f32[1120,256]{1,0:T(8,128)}, u32[]{:S(2)}, u32[]{:S(2)}) collective-permute-start(f32[1120,256]{1,0:T(8,128)S(1)} %slice.6.refs_0_), channel_id=1, source_target_pairs={{0,2},{8,10},{16,18},{24,26},{32,34},{40,42},{48,50},{56,58},{64,6... | collective-permute-start | bytes 3440648 | tf_op jit(solution)/shard_map/ppermute | solution.py:317
  3.3 1.3 %slice.7.refs_1_ = f32[928,256]{1,0:T(8,128)S(1)} slice(f32[2048,1024]{1,0:T(8,128)} %matrix.5), slice={[1120:2048], [0:256]} | slice | bytes 1900544 | tf_op jit(solution)/shard_map/slice | solution.py:316
  4.5 1.6 %collective-permute-start.3 = (f32[928,256]{1,0:T(8,128)S(1)}, f32[928,256]{1,0:T(8,128)}, u32[]{:S(2)}, u32[]{:S(2)}) collective-permute-start(f32[928,256]{1,0:T(8,128)S(1)} %slice.7.refs_1_), channel_id=1, source_target_pairs={{0,6},{8,14},{16,22},{24,30},{32,38},{40,46},{48,54},{56,62},{64,7... | collective-permute-start | bytes 2850824 | tf_op jit(solution)/shard_map/ppermute | solution.py:318
  6.2 1.7 %collective-permute-start.5 = (f32[1120,256]{1,0:T(8,128)S(1)}, f32[1120,256]{1,0:T(8,128)}, u32[]{:S(2)}, u32[]{:S(2)}) collective-permute-start(f32[1120,256]{1,0:T(8,128)S(1)} %slice.6.refs_0_), channel_id=1, source_target_pairs={{0,6},{8,14},{16,22},{24,30},{32,38},{40,46},{48,54},{56,62},{64,7... | collective-permute-start | bytes 3440648 | tf_op jit(solution)/shard_map/ppermute | solution.py:319
  7.8 12.0 %collective-permute-done.refs_2_ = f32[1120,256]{1,0:T(8,128)} collective-permute-done((f32[1120,256]{1,0:T(8,128)S(1)}, f32[1120,256]{1,0:T(8,128)}, u32[]{:S(2)}, u32[]{:S(2)}) %collective-permute-start) | collective-permute-done | bytes 1146912 | tf_op jit(solution)/shard_map/ppermute | solution.py:317
  19.8 2.3 %collective-permute-start.2 = (f32[1120,256]{1,0:T(8,128)}, f32[1120,256]{1,0:T(8,128)}, u32[]{:S(2)}, u32[]{:S(2)}) collective-permute-start(f32[1120,256]{1,0:T(8,128)} %collective-permute-done.refs_2_), channel_id=1, source_target_pairs={{2,4},{10,12},{18,20},{26,28},{34,36},{42,44},{50,52},{58,60},{66,... | collective-permute-start | bytes 3440648 | tf_op jit(solution)/shard_map/ppermute | solution.py:323
  22.1 1.3 %collective-permute-start.1 = (f32[928,256]{1,0:T(8,128)S(1)}, f32[928,256]{1,0:T(8,128)}, u32[]{:S(2)}, u32[]{:S(2)}) collective-permute-start(f32[928,256]{1,0:T(8,128)S(1)} %slice.7.refs_1_), channel_id=1, source_target_pairs={{0,2},{8,10},{16,18},{24,26},{32,34},{40,42},{48,50},{56,58},{64,6... | collective-permute-start | bytes 2850824 | tf_op jit(solution)/shard_map/ppermute | solution.py:320
  23.4 0.0 collective-permute-done.3.refs_7_
  23.4 1.6 %collective-permute-start.4 = (f32[928,256]{1,0:T(8,128)}, f32[928,256]{1,0:T(8,128)}, u32[]{:S(2)}, u32[]{:S(2)}) collective-permute-start(f32[928,256]{1,0:T(8,128)} %collective-permute-done.3.refs_7_), channel_id=1, source_target_pairs={{6,4},{14,12},{22,20},{30,28},{38,36},{46,44},{54,52},{62,60},{70,... | collective-permute-start | bytes 2850824 | tf_op jit(solution)/shard_map/ppermute | solution.py:324
  25.0 0.1 pad_add_fusion.place
  25.1 0.0 copy-start
  25.1 12.7 %collective-permute-done.1.refs_3_ = f32[928,256]{1,0:T(8,128)} collective-permute-done((f32[928,256]{1,0:T(8,128)S(1)}, f32[928,256]{1,0:T(8,128)}, u32[]{:S(2)}, u32[]{:S(2)}) %collective-permute-start.1) | collective-permute-done | bytes 950304 | tf_op jit(solution)/shard_map/ppermute | solution.py:320
  37.8 0.0 collective-permute-done.5.refs_6_
  37.9 0.0 collective-permute-done.4.refs_5_
  37.9 0.0 collective-permute-done.2.refs_4_
  37.9 2.1 %shard_map.30.panel_here = f32[2048,256]{1,0:T(8,128)S(1)} custom-call(s32[4]{0:T(128)S(1)} %pad_add_fusion.place, f32[1120,256]{1,0:T(8,128)S(1)} %slice.6.refs_0_, f32[928,256]{1,0:T(8,128)S(1)} %slice.7.refs_1_, f32[1120,256]{1,0:T(8,128)} %collective-permute-done.refs_2_, f32[928,256]{1,0:T(8,128)} %collective-permute-done.1.refs_3_, ...), custom_call_target="tpu_custom_call" | custom-call | flops 100000000 | bytes 4194304 | tf_op jit(solution)/shard_map/pallas_call | solution.py:234
  40.0 1.4 %collective-permute-start.6 = (f32[2048,256]{1,0:T(8,128)S(1)}, f32[2048,256]{1,0:T(8,128)S(1)}, u32[]{:S(2)}, u32[]{:S(2)}) collective-permute-start(f32[2048,256]{1,0:T(8,128)S(1)} %shard_map.30.panel_here), channel_id=1, source_target_pairs={{0,1},{2,3},{4,5},{6,7},{8,9},{10,11},{12,13},{14,15},{16,17},{18,... | collective-permute-start | bytes 6291464 | tf_op jit(solution)/shard_map/ppermute | solution.py:326
  41.4 0.0 copy-done
  41.4 0.7 shard_map.31
  42.1 0.7 shard_map.32
  42.8 2.3 %collective-permute-done.6.panel_sent = f32[2048,256]{1,0:T(8,128)S(1)} collective-permute-done((f32[2048,256]{1,0:T(8,128)S(1)}, f32[2048,256]{1,0:T(8,128)S(1)}, u32[]{:S(2)}, u32[]{:S(2)}) %collective-permute-start.6) | collective-permute-done | bytes 2097184 | tf_op jit(solution)/shard_map/ppermute | solution.py:326
  45.1 5.3 %shard_map.33 = (f32[256,1280]{1,0:T(8,128)S(1)}, bf16[2048,256]{1,0:T(8,128)(2,1)S(1)}, bf16[2048,256]{1,0:T(8,128)(2,1)S(1)}) custom-call(s32[4]{0:T(128)S(1)} %pad_add_fusion.place, f32[2048,256]{1,0:T(8,128)S(1)} %shard_map.30.panel_here, f32[2048,256]{1,0:T(8,128)S(1)} %collective-permute-done.6.panel_sent, ...), custom_call_target="tpu_custom_call" | custom-call | flops 5000000000 | bytes 16777216 | tf_op jit(solution)/shard_map/pallas_call | solution.py:248
  50.3 27.1 %all_to_all.10.tiles = f32[16,16,1280]{2,1,0:T(8,128)S(1)} all-to-all(f32[16,16,1280]{2,1,0:T(8,128)S(1)} %bitcast.6), channel_id=1, replica_groups=mesh['row'=16,'z'=4,'c'=2] {'row'}, dimensions={0} | all-to-all | bytes 2621440 | tf_op jit(solution)/shard_map/all_to_all | solution.py:294
  77.5 0.1 shard_map.34
  77.6 22.6 %all_to_all.11 = f32[16,16,1280]{2,1,0:T(8,128)S(1)} all-to-all(f32[16,16,1280]{2,1,0:T(8,128)S(1)} %shard_map.34), channel_id=1, replica_groups=mesh['row'=16,'z'=4,'c'=2] {'row'}, dimensions={0} | all-to-all | bytes 2621440 | tf_op jit(solution)/shard_map/all_to_all | solution.py:294
  100.2 15.3 %shard_map.35 = (f32[16,1024]{1,0:T(8,128)}, f32[2048,1024]{1,0:T(8,128)}) custom-call(s32[4]{0:T(128)S(1)} %pad_add_fusion.place, f32[256,1280]{1,0:T(8,128)S(1)} %bitcast.7, bf16[2048,256]{1,0:T(8,128)(2,1)S(1)} %get-tuple-element.14.panel_high, bf16[2048,256]{1,0:T(8,128)(2,1)S(1)} %get-tuple-element.15.panel_low, f32[2048,1024]{1,0:T(8,128)} %matrix.5), custom_call_target="tpu_custom_call" | custom-call | flops 8000000000 | bytes 25165824 | tf_op jit(solution)/shard_map/pallas_call | solution.py:260
Async XLA Ops:
  2.0 17.9 %collective-permute-start = (f32[1120,256]{1,0:T(8,128)S(1)}, f32[1120,256]{1,0:T(8,128)}, u32[]{:S(2)}, u32[]{:S(2)}) collective-permute-start(f32[1120,256]{1,0:T(8,128)S(1)} %slice.6.refs_0_), channel_id=1, source_target_pairs={{0,2},{8,10},{16,18},{24,26},{32,34},{40,42},{48,50},{56,58},{64,6... | collective-permute-start | bytes 3440648 | tf_op jit(solution)/shard_map/ppermute | solution.py:317
  4.5 18.9 %collective-permute-start.3 = (f32[928,256]{1,0:T(8,128)S(1)}, f32[928,256]{1,0:T(8,128)}, u32[]{:S(2)}, u32[]{:S(2)}) collective-permute-start(f32[928,256]{1,0:T(8,128)S(1)} %slice.7.refs_1_), channel_id=1, source_target_pairs={{0,6},{8,14},{16,22},{24,30},{32,38},{40,46},{48,54},{56,62},{64,7... | collective-permute-start | bytes 2850824 | tf_op jit(solution)/shard_map/ppermute | solution.py:318
  6.2 31.7 %collective-permute-start.5 = (f32[1120,256]{1,0:T(8,128)S(1)}, f32[1120,256]{1,0:T(8,128)}, u32[]{:S(2)}, u32[]{:S(2)}) collective-permute-start(f32[1120,256]{1,0:T(8,128)S(1)} %slice.6.refs_0_), channel_id=1, source_target_pairs={{0,6},{8,14},{16,22},{24,30},{32,38},{40,46},{48,54},{56,62},{64,7... | collective-permute-start | bytes 3440648 | tf_op jit(solution)/shard_map/ppermute | solution.py:319
  19.8 18.0 %collective-permute-start.2 = (f32[1120,256]{1,0:T(8,128)}, f32[1120,256]{1,0:T(8,128)}, u32[]{:S(2)}, u32[]{:S(2)}) collective-permute-start(f32[1120,256]{1,0:T(8,128)} %collective-permute-done.refs_2_), channel_id=1, source_target_pairs={{2,4},{10,12},{18,20},{26,28},{34,36},{42,44},{50,52},{58,60},{66,... | collective-permute-start | bytes 3440648 | tf_op jit(solution)/shard_map/ppermute | solution.py:323
  22.1 15.7 %collective-permute-start.1 = (f32[928,256]{1,0:T(8,128)S(1)}, f32[928,256]{1,0:T(8,128)}, u32[]{:S(2)}, u32[]{:S(2)}) collective-permute-start(f32[928,256]{1,0:T(8,128)S(1)} %slice.7.refs_1_), channel_id=1, source_target_pairs={{0,2},{8,10},{16,18},{24,26},{32,34},{40,42},{48,50},{56,58},{64,6... | collective-permute-start | bytes 2850824 | tf_op jit(solution)/shard_map/ppermute | solution.py:320
  23.4 14.4 %collective-permute-start.4 = (f32[928,256]{1,0:T(8,128)}, f32[928,256]{1,0:T(8,128)}, u32[]{:S(2)}, u32[]{:S(2)}) collective-permute-start(f32[928,256]{1,0:T(8,128)} %collective-permute-done.3.refs_7_), channel_id=1, source_target_pairs={{6,4},{14,12},{22,20},{30,28},{38,36},{46,44},{54,52},{62,60},{70,... | collective-permute-start | bytes 2850824 | tf_op jit(solution)/shard_map/ppermute | solution.py:324
  25.1 16.3 %copy-start = (f32[2048,1024]{1,0:T(8,128)S(1)}, f32[2048,1024]{1,0:T(8,128)}, u32[]{:S(2)}) copy-start(f32[2048,1024]{1,0:T(8,128)} %matrix.5) | copy-start | bytes 25165828
  40.0 5.1 %collective-permute-start.6 = (f32[2048,256]{1,0:T(8,128)S(1)}, f32[2048,256]{1,0:T(8,128)S(1)}, u32[]{:S(2)}, u32[]{:S(2)}) collective-permute-start(f32[2048,256]{1,0:T(8,128)S(1)} %shard_map.30.panel_here), channel_id=1, source_target_pairs={{0,1},{2,3},{4,5},{6,7},{8,9},{10,11},{12,13},{14,15},{16,17},{18,... | collective-permute-start | bytes 6291464 | tf_op jit(solution)/shard_map/ppermute | solution.py:326
